TPU v7x, 8 devices: a whole 2x2x1 slice. The times are simulated.
8 devices in a mesh: dp: 1 (over z), ep: 8 (over y, x, core).
Axes of the slice: x: 2, y: 2, z: 1, core: 2. Of those that a mesh axis runs over, the one named last changes fastest.
Arguments:
- hidden: bfloat16 [2048, 2560], P(('dp', 'ep'))
- norm_gain: bfloat16 [2560], replicated
- w_gate: bfloat16 [2560, 64], replicated
- w1_shared: bfloat16 [2560, 3072], replicated
- w3_shared: bfloat16 [2560, 3072], replicated
- w2_shared: bfloat16 [3072, 2560], replicated
- w1_experts: bfloat16 [64, 2560, 1536], P('ep')
- w3_experts: bfloat16 [64, 2560, 1536], P('ep')
- w2_experts: bfloat16 [64, 1536, 2560], P('ep')
- topk_ids: int32 [2048, 6], P(('dp', 'ep'))
Outputs:
- output: bfloat16 [2048, 2560], P(('dp', 'ep'))
All inputs are finite; a program needn't handle non-finite values.
Results may differ from a plain program's by a relative error of at most 0.00584073.
Values are sent between devices in bfloat16 or wider.
A program may use at most 1 GiB of HBM per device.

v0:
```python
import functools

import jax
import jax.numpy as jnp
from jax import lax
from jax.experimental import pallas as pl
from jax.experimental.pallas import tpu as pltpu
from jax.sharding import PartitionSpec as P

ROUTE_SCALE = 16
NORM_EPS = 1e-6
D = 2560
FF = 1536
EXPERTS = 64
NE = 8
NSB = 4
SB = 512
G = 16
TM = 256
XG = 432
XR = XG * G
SBR = 1792
FC = 512
NF = FF // FC
T = 256
SHARED = 3072
SF = 256
CW = 512
RC = 256
NC = D // RC
VMEM_LIMIT = 66000000
BF16 = jnp.bfloat16
F32 = jnp.float32


def rms_norm(hidden, norm_gain):
    rows_f = hidden.astype(F32)
    inv_rms = lax.rsqrt(jnp.mean(rows_f * rows_f, axis=-1, keepdims=True) + NORM_EPS)
    return (rows_f * inv_rms * norm_gain.astype(F32)).astype(BF16)


def offsets(cnt_ref, ng, eoff, est, boff, nsb_g):
    run = jnp.int32(0)
    for e in range(NE):
        est[e] = run
        for s in range(NSB):
            n = (cnt_ref[s, e] + (G - 1)) // G
            ng[s * NE + e] = n
            eoff[s * NE + e] = run
            run = run + n
    est[NE] = run
    for s in range(NSB):
        b = jnp.int32(0)
        for e in range(NE):
            boff[s * NE + e] = b
            b = b + ng[s * NE + e]
        nsb_g[s] = b


def up_kernel(cnt_ref, rank_ref, ball, w1, w3, h_out, xs, bbuf, pbuf, tbuf, wbuf, hbuf, ng, eoff, est, boff, nsb_g, dst, last, bsem, wsem, hsem):
    def w_copies(step, slot):
        e = step // NF
        f = step % NF
        cols = pl.ds(pl.multiple_of(f * FC, FC), FC)
        return (pltpu.make_async_copy(w1.at[e, :, cols], wbuf.at[slot, 0], wsem.at[slot, 0]),
                pltpu.make_async_copy(w3.at[e, :, cols], wbuf.at[slot, 1], wsem.at[slot, 1]))

    def b_copy(s, slot):
        return pltpu.make_async_copy(ball.at[pl.ds(s * SB, SB), :], bbuf.at[slot], bsem.at[slot])

    b_copy(0, 0).start()
    for c in w_copies(0, 0):
        c.start()
    for c in w_copies(1, 1):
        c.start()
    offsets(cnt_ref, ng, eoff, est, boff, nsb_g)
    rows16 = lax.broadcasted_iota(jnp.int32, (G, SB), 0)

    for s in range(NSB):
        slot = s % 2
        if s + 1 < NSB:
            b_copy(s + 1, 1 - slot).start()
        for e in range(NE):
            rk = jnp.broadcast_to(rank_ref[s, e:e + 1, :], (G, SB))

            def build(g, _, s=s, e=e, rk=rk):
                k = boff[s * NE + e] + g
                dst[k] = eoff[s * NE + e] + g
                hit = jnp.where(rk == rows16 + g * G, 1.0, 0.0)
                pbuf[pl.ds(pl.multiple_of(k * G, G), G), :] = hit.astype(BF16)
                return 0

            lax.fori_loop(0, ng[s * NE + e], build, 0)
        b_copy(s, slot).wait()

        def tile(m, _, s=s, slot=slot):
            prow = pbuf[pl.ds(pl.multiple_of(m * TM, TM), TM), :]
            for n in range(D // 512):
                cols = slice(n * 512, (n + 1) * 512)
                tbuf[:, cols] = jnp.dot(prow, bbuf[slot, :, cols], preferred_element_type=F32).astype(BF16)

            def put(j, _):
                row = pl.multiple_of(dst[m * (TM // G) + j] * G, G)
                xs[pl.ds(row, G), :] = tbuf[pl.ds(pl.multiple_of(j * G, G), G), :]
                return 0

            lax.fori_loop(0, jnp.minimum(TM // G, nsb_g[s] - m * (TM // G)), put, 0)
            return 0

        lax.fori_loop(0, (nsb_g[s] + TM // G - 1) // (TM // G), tile, 0)

    def h_copy(hs, row, col, size):
        return pltpu.make_async_copy(hbuf.at[hs, pl.ds(0, size), :], h_out.at[pl.ds(row, size), pl.ds(col, FC)], hsem.at[0])

    def wait_h(quarters):
        for q in range(1, 5):
            @pl.when(quarters == q)
            def _(q=q):
                h_copy(0, 0, 0, q * 64).wait()

    def step(st, k):
        slot = st % 2
        e = st // NF
        col = pl.multiple_of((st % NF) * FC, FC)
        for c in w_copies(st, slot):
            c.wait()
        base = est[e] * G
        rows = est[e + 1] * G - base

        def work(row, size, k):
            row = pl.multiple_of(row, G)
            hs = k % 2
            x = xs[pl.ds(row, size), :]
            gate = jnp.dot(x, wbuf[slot, 0], preferred_element_type=F32)
            lin = jnp.dot(x, wbuf[slot, 1], preferred_element_type=F32)
            hbuf[hs, pl.ds(0, size), :] = (jax.nn.silu(gate) * lin).astype(BF16)

            @pl.when(k > 0)
            def _():
                wait_h(last[0])

            last[0] = size // 64
            h_copy(hs, row, col, size).start()

        full = rows // TM

        def body(m, k):
            work(base + m * TM, TM, k)
            return k + 1

        k = lax.fori_loop(0, full, body, k)
        rem = rows - full * TM
        at = base + full * TM
        for size in (64, 128, 192, 256):
            @pl.when((rem > size - 64) & (rem <= size))
            def _(size=size):
                work(at, size, k)

        @pl.when(st + 2 < NE * NF)
        def _():
            for c in w_copies(st + 2, slot):
                c.start()

        return k + jnp.where(rem > 0, 1, 0)

    @pl.when(lax.fori_loop(0, NE * NF, step, jnp.int32(0)) > 0)
    def _():
        wait_h(last[0])


def up_call(cnt, rank, ball, w1, w3):
    any_spec = pl.BlockSpec(memory_space=pl.ANY)
    return pl.pallas_call(
        up_kernel,
        out_shape=jax.ShapeDtypeStruct((XR, FF), BF16),
        in_specs=[pl.BlockSpec(memory_space=pltpu.SMEM), pl.BlockSpec(memory_space=pltpu.VMEM), any_spec, any_spec, any_spec],
        out_specs=any_spec,
        scratch_shapes=[
            pltpu.VMEM((XR, D), BF16),
            pltpu.VMEM((2, SB, D), BF16),
            pltpu.VMEM((SBR, SB), BF16),
            pltpu.VMEM((TM, D), BF16),
            pltpu.VMEM((2, 2, D, FC), BF16),
            pltpu.VMEM((2, TM, FC), BF16),
            pltpu.SMEM((NSB * NE,), jnp.int32),
            pltpu.SMEM((NSB * NE,), jnp.int32),
            pltpu.SMEM((NE + 1,), jnp.int32),
            pltpu.SMEM((NSB * NE,), jnp.int32),
            pltpu.SMEM((NSB,), jnp.int32),
            pltpu.SMEM((SBR // G,), jnp.int32),
            pltpu.SMEM((1,), jnp.int32),
            pltpu.SemaphoreType.DMA((2,)),
            pltpu.SemaphoreType.DMA((2, 2)),
            pltpu.SemaphoreType.DMA((1,)),
        ],
        compiler_params=pltpu.CompilerParams(vmem_limit_bytes=VMEM_LIMIT),
        cost_estimate=pl.CostEstimate(flops=48_000_000_000, bytes_accessed=140_000_000, transcendentals=0),
        name="up",
    )(cnt, rank, ball, w1, w3)


def down_kernel(cnt_ref, core_ref, rank_ref, wt_ref, h, w2, mine, theirs,
                hs, ebuf, kbuf, pbuf, wbuf, abuf, wsplit, ng, eoff, est, boff, nsb_g, hsem, wsem, osem):
    steps = (D // CW) * NE

    def w_copy(st, slot):
        col = pl.multiple_of((st // NE) * CW, CW)
        return pltpu.make_async_copy(w2.at[st % NE, :, pl.ds(col, CW)], wbuf.at[slot], wsem.at[slot])

    def h_copy(t):
        rows = pl.ds(pl.multiple_of(t * TM, TM), TM)
        return pltpu.make_async_copy(h.at[rows, :], hs.at[rows, :], hsem.at[0])

    for st in range(3):
        w_copy(st, st).start()
    offsets(cnt_ref, ng, eoff, est, boff, nsb_g)
    nh = (est[NE] + TM // G - 1) // (TM // G)

    def h_start(t, _):
        h_copy(t).start()
        return 0

    def h_wait(t, _):
        h_copy(t).wait()
        return 0

    lax.fori_loop(0, nh, h_start, 0)
    for s in range(NSB):
        w = wt_ref[s]
        hi = w.astype(BF16).astype(F32)
        mid = (w - hi).astype(BF16).astype(F32)
        wsplit[0, s] = hi
        wsplit[1, s] = mid
        wsplit[2, s] = w - hi - mid
    rows16 = lax.broadcasted_iota(jnp.int32, (G, SB), 0)
    for s in range(NSB):
        for e in range(NE):
            rk = jnp.broadcast_to(rank_ref[s, e:e + 1, :], (G, SB))
            parts = [jnp.broadcast_to(wsplit[i, s, e:e + 1, :], (G, SB)) for i in range(3)]

            def build(g, _, s=s, e=e, rk=rk, parts=parts):
                row = pl.multiple_of((boff[s * NE + e] + g) * G, G)
                hit = rk == rows16 + g * G
                for i in range(3):
                    pbuf[s, i, pl.ds(row, G), :] = jnp.where(hit, parts[i], 0.0).astype(BF16)
                return 0

            lax.fori_loop(0, ng[s * NE + e], build, 0)

        def clear(g, _, s=s):
            row = pl.multiple_of(g * G, G)
            for i in range(3):
                pbuf[s, i, pl.ds(row, G), :] = jnp.zeros((G, SB), BF16)
            return 0

        lax.fori_loop(nsb_g[s], -(-nsb_g[s] // (TM // G)) * (TM // G), clear, 0)
    kbuf[...] = jnp.zeros_like(kbuf)
    lax.fori_loop(0, nh, h_wait, 0)

    core = core_ref[0]

    def out_copies(c, s, slot):
        rel = core_ref[1 + s]
        keep = pl.multiple_of(core * 256, 256)
        give = pl.multiple_of(256 - core * 256, 256)
        out = []
        for i in range(CW // RC):
            cols = pl.ds(i * RC, RC)
            j = c * (CW // RC) + i
            out.append(pltpu.make_async_copy(abuf.at[slot, pl.ds(give, 256), cols], theirs.at[j, rel], osem.at[slot, i, 0]))
            out.append(pltpu.make_async_copy(abuf.at[slot, pl.ds(keep, 256), cols], mine.at[j, rel], osem.at[slot, i, 1]))
        return out

    def column(c, _):
        def expert(e, _):
            st = c * NE + e
            ws = st % 3
            w_copy(st, ws).wait()
            base = est[e] * G
            rows = est[e + 1] * G - base

            def work(row, size):
                row = pl.multiple_of(row, G)
                ebuf[pl.ds(row, size), :] = jnp.dot(hs[pl.ds(row, size), :], wbuf[ws], preferred_element_type=F32).astype(BF16)

            full = rows // TM

            def body(m, _):
                work(base + m * TM, TM)
                return 0

            lax.fori_loop(0, full, body, 0)
            rem = rows - full * TM
            for size in (64, 128, 192, 256):
                @pl.when((rem > size - 64) & (rem <= size))
                def _(size=size):
                    work(base + full * TM, size)

            @pl.when(st + 3 < steps)
            def _():
                w_copy(st + 3, ws).start()

            return 0

        lax.fori_loop(0, NE, expert, 0)

        def block(s, _):
            slot = s % 2

            def segment(e, _):
                def move(g, _):
                    row = pl.multiple_of((boff[s * NE + e] + g) * G, G)
                    src = pl.multiple_of((eoff[s * NE + e] + g) * G, G)
                    kbuf[pl.ds(row, G), :] = ebuf[pl.ds(src, G), :]
                    return 0

                return lax.fori_loop(0, ng[s * NE + e], move, 0)

            lax.fori_loop(0, NE, segment, 0)
            nk = (nsb_g[s] + TM // G - 1) // (TM // G)

            @pl.when(c * NSB + s >= 2)
            def _():
                for cp in out_copies(c, s, slot):
                    cp.wait()

            abuf[slot] = jnp.zeros((SB, CW), F32)

            def tile(kt, _):
                rows = pl.ds(pl.multiple_of(kt * TM, TM), TM)
                ek = kbuf[rows, :]
                for half in range(2):
                    toks = slice(half * 256, half * 256 + 256)
                    tot = abuf[slot, toks, :]
                    for i in range(3):
                        tot = tot + lax.dot_general(pbuf[s, i, rows, toks], ek, (((0,), (0,)), ((), ())), preferred_element_type=F32)
                    abuf[slot, toks, :] = tot
                return 0

            lax.fori_loop(0, nk, tile, 0)
            for cp in out_copies(c, s, slot):
                cp.start()
            return 0

        return lax.fori_loop(0, NSB, block, 0)

    lax.fori_loop(0, D // CW, column, 0)
    for s in (NSB - 2, NSB - 1):
        for cp in out_copies(D // CW - 1, s, s % 2):
            cp.wait()


def down_call(cnt, core, rank, wts, h, w2):
    any_spec = pl.BlockSpec(memory_space=pl.ANY)
    smem = pl.BlockSpec(memory_space=pltpu.SMEM)
    vmem = pl.BlockSpec(memory_space=pltpu.VMEM)
    out = jax.ShapeDtypeStruct((NC, NSB, 256, RC), F32)
    return pl.pallas_call(
        down_kernel,
        out_shape=(out, out),
        in_specs=[smem, smem, vmem, vmem, any_spec, any_spec],
        out_specs=(any_spec, any_spec),
        scratch_shapes=[
            pltpu.VMEM((XR, FF), BF16),
            pltpu.VMEM((XR, CW), BF16),
            pltpu.VMEM((SBR, CW), BF16),
            pltpu.VMEM((NSB, 3, SBR, SB), BF16),
            pltpu.VMEM((3, FF, CW), BF16),
            pltpu.VMEM((2, SB, CW), F32),
            pltpu.VMEM((3, NSB, NE, SB), F32),
            pltpu.SMEM((NSB * NE,), jnp.int32),
            pltpu.SMEM((NSB * NE,), jnp.int32),
            pltpu.SMEM((NE + 1,), jnp.int32),
            pltpu.SMEM((NSB * NE,), jnp.int32),
            pltpu.SMEM((NSB,), jnp.int32),
            pltpu.SemaphoreType.DMA((1,)),
            pltpu.SemaphoreType.DMA((3,)),
            pltpu.SemaphoreType.DMA((2, CW // RC, 2)),
        ],
        compiler_params=pltpu.CompilerParams(vmem_limit_bytes=VMEM_LIMIT),
        cost_estimate=pl.CostEstimate(flops=40_000_000_000, bytes_accessed=100_000_000, transcendentals=0),
        name="down",
    )(cnt, core, rank, wts, h, w2)


def neighbours():
    me = lax.axis_index('ep')
    core = me + 1 - 2 * (me % 2)
    x = me + 2 - 4 * ((me // 2) % 2)
    y = me + 4 - 8 * (me // 4)
    return me, core, x, y


def remote(src, dst, send, recv, dev):
    return pltpu.make_async_remote_copy(src_ref=src, dst_ref=dst, send_sem=send, recv_sem=recv, device_id={'ep': dev}, device_id_type=pl.DeviceIdType.MESH)


def enter(others):
    barrier = pltpu.get_barrier_semaphore()
    for dev in others:
        pl.semaphore_signal(barrier, inc=1, device_id={'ep': dev}, device_id_type=pl.DeviceIdType.MESH)
    pl.semaphore_wait(barrier, len(others))


def gather_kernel(b_any, b_ref, wts_ref, w1, w3, w2, ball, wall, s_ref, w13buf, w2buf, acc, send, recv, wsend, wrecv, local, wsem):
    me, pn, xn, yn = neighbours()
    diag = xn + yn - me
    half = T // 2

    def rows(dev, h):
        return pl.ds(pl.multiple_of(dev * T + h * half, half), half)

    def own(k, h, dev):
        return remote(b_any.at[pl.ds(h * half, half), :], ball.at[rows(me, h), :], send.at[k], recv.at[k], dev)

    def relay(k, owner, h, dev):
        return remote(ball.at[rows(owner, h), :], ball.at[rows(owner, h), :], send.at[k], recv.at[k], dev)

    def w_copies(st, slot):
        cols = pl.ds(pl.multiple_of(st * SF, SF), SF)
        return (pltpu.make_async_copy(w1.at[:, cols], w13buf.at[slot, 0], wsem.at[slot, 0]),
                pltpu.make_async_copy(w3.at[:, cols], w13buf.at[slot, 1], wsem.at[slot, 1]),
                pltpu.make_async_copy(w2.at[cols, :], w2buf.at[slot], wsem.at[slot, 2]))

    for st in range(3):
        for c in w_copies(st, st):
            c.start()
    others = [lax.rem(me + k, 8) for k in range(1, 8)]
    enter(others)
    first = [own(0, 0, xn), own(2, 1, yn), own(1, 1, xn), own(3, 0, yn), own(4, 0, pn), own(5, 1, pn)]
    for c in first:
        c.start()
    lanes = pl.ds(pl.multiple_of((me % 2) * T, T), T)
    small = []
    for k, dev in enumerate(others):
        small.append(remote(wts_ref.at[pl.ds(pl.multiple_of(dev * NE, NE), NE), :], wall.at[me // 2, :, lanes], wsend.at[k], wrecv.at[k], dev))
        small[-1].start()
    keep = [pltpu.make_async_copy(b_ref, ball.at[pl.ds(pl.multiple_of(me * T, T), T), :], local.at[0]),
            pltpu.make_async_copy(wts_ref.at[pl.ds(pl.multiple_of(me * NE, NE), NE), :], wall.at[me // 2, :, lanes], local.at[1])]
    for c in keep:
        c.start()
    acc[...] = jnp.zeros_like(acc)

    def step(st, _):
        slot = lax.rem(st, 3)
        for c in w_copies(st, slot):
            c.wait()
        x = b_ref[...]
        gate = jnp.dot(x, w13buf[slot, 0], preferred_element_type=F32)
        lin = jnp.dot(x, w13buf[slot, 1], preferred_element_type=F32)
        inner = (jax.nn.silu(gate) * lin).astype(BF16)
        for n in range(D // 512):
            cols = slice(n * 512, n * 512 + 512)
            acc[:, cols] += jnp.dot(inner, w2buf[slot, :, cols], preferred_element_type=F32)

        return 0

    def refill(st, _):
        step(st, 0)
        for c in w_copies(st + 3, lax.rem(st, 3)):
            c.start()
        return 0

    lax.fori_loop(0, 8, refill, 0)
    first[0].wait_recv()
    first[1].wait_recv()
    second = [relay(6, xn, 0, yn), relay(7, yn, 1, xn), relay(8, xn, 0, pn), relay(9, yn, 1, pn)]
    for c in second:
        c.start()
    lax.fori_loop(8, SHARED // SF - 3, refill, 0)
    lax.fori_loop(SHARED // SF - 3, SHARED // SF, step, 0)
    s_ref[...] = acc[...].astype(BF16)
    first[2].wait_recv()
    first[3].wait_recv()
    third = [relay(10, xn, 1, pn), relay(11, yn, 0, pn)]
    for c in third:
        c.start()
    second[0].wait_recv()
    second[1].wait_recv()
    fourth = [relay(12, diag, 0, pn), relay(13, diag, 1, pn)]
    for c in fourth:
        c.start()
    for c in (first[4], first[5], second[2], second[3], *third, *fourth):
        c.wait_recv()
    for c in (*first, *second, *third, *fourth):
        c.wait_send()
    for c in small:
        c.wait()
    for c in keep:
        c.wait()


def gather_call(b, wts, w1, w3, w2):
    any_spec = pl.BlockSpec(memory_space=pl.ANY)
    vmem = pl.BlockSpec(memory_space=pltpu.VMEM)
    return pl.pallas_call(
        gather_kernel,
        out_shape=(jax.ShapeDtypeStruct((8 * T, D), BF16), jax.ShapeDtypeStruct((NSB, NE, SB), F32), jax.ShapeDtypeStruct((T, D), BF16)),
        in_specs=[any_spec, vmem, vmem, any_spec, any_spec, any_spec],
        out_specs=(any_spec, any_spec, vmem),
        scratch_shapes=[
            pltpu.VMEM((3, 2, D, SF), BF16),
            pltpu.VMEM((3, SF, D), BF16),
            pltpu.VMEM((T, D), F32),
            pltpu.SemaphoreType.DMA((14,)),
            pltpu.SemaphoreType.DMA((14,)),
            pltpu.SemaphoreType.DMA((7,)),
            pltpu.SemaphoreType.DMA((7,)),
            pltpu.SemaphoreType.DMA((2,)),
            pltpu.SemaphoreType.DMA((3, 3)),
        ],
        compiler_params=pltpu.CompilerParams(collective_id=0, has_side_effects=True, vmem_limit_bytes=VMEM_LIMIT),
        cost_estimate=pl.CostEstimate(flops=12_000_000_000, bytes_accessed=60_000_000, transcendentals=0),
        name="gather",
    )(b, b, wts, w1, w3, w2)


def return_kernel(mine, theirs, y_ref, s_ref, out_ref, own, r1, r2x, r2y, r3x, r3y, send, recv, load):
    me, pn, xn, yn = neighbours()
    half = T // 2
    top, low = pl.ds(0, half), pl.ds(half, half)

    def load_of(j):
        return pltpu.make_async_copy(mine.at[j], own.at[j], load.at[j])

    def core_of(j):
        return remote(theirs.at[j], r1.at[j], send.at[0, j], recv.at[0, j], pn)

    def x_of(j):
        return remote(own.at[j, pl.ds(1, 2), top, :], r2x.at[j], send.at[1, j], recv.at[1, j], xn)

    def y_of(j):
        return remote(own.at[j, pl.ds(2, 2), low, :], r2y.at[j], send.at[2, j], recv.at[2, j], yn)

    def y_last(j):
        return remote(own.at[j, 3, top, :], r3y.at[j], send.at[3, j], recv.at[3, j], yn)

    def x_last(j):
        return remote(own.at[j, 1, low, :], r3x.at[j], send.at[4, j], recv.at[4, j], xn)

    def each(body):
        def run(j, _):
            body(j)
            return 0

        lax.fori_loop(0, NC, run, 0)

    def begin(j):
        load_of(j).start()
        core_of(j).start()

    def pair(j):
        load_of(j).wait()
        core_of(j).wait_recv()
        own[j, 1:] = own[j, 1:] + r1[j, 1:]
        x_of(j).start()
        y_of(j).start()
        own[j, 0] = own[j, 0] + r1[j, 0]

    def onward(j):
        x_of(j).wait_recv()
        own[j, 3, :half] = own[j, 3, :half] + r2x[j, 1]
        y_last(j).start()
        y_of(j).wait_recv()
        own[j, 1, half:] = own[j, 1, half:] + r2y[j, 0]
        x_last(j).start()

    def finish(j):
        cols = pl.ds(pl.multiple_of(j * RC, RC), RC)
        y_last(j).wait_recv()
        x_last(j).wait_recv()
        base = y_ref[:, cols].astype(F32) + s_ref[:, cols].astype(F32)
        out_ref[:half, cols] = (base[:half] + (own[j, 0, :half] + r2x[j, 0] + r3y[j])).astype(BF16)
        out_ref[half:, cols] = (base[half:] + (own[j, 0, half:] + r2y[j, 1] + r3x[j])).astype(BF16)

    def drain(j):
        for c in (core_of(j), x_of(j), y_of(j), y_last(j), x_last(j)):
            c.wait_send()

    enter([pn, xn, yn])
    each(begin)
    each(pair)
    each(onward)
    each(finish)
    each(drain)


def return_call(mine, theirs, hidden, shared_out):
    any_spec = pl.BlockSpec(memory_space=pl.ANY)
    vmem = pl.BlockSpec(memory_space=pltpu.VMEM)
    half = T // 2
    return pl.pallas_call(
        return_kernel,
        out_shape=jax.ShapeDtypeStruct((T, D), BF16),
        in_specs=[any_spec, any_spec, vmem, vmem],
        out_specs=vmem,
        scratch_shapes=[
            pltpu.VMEM((NC, NSB, T, RC), F32),
            pltpu.VMEM((NC, NSB, T, RC), F32),
            pltpu.VMEM((NC, 2, half, RC), F32),
            pltpu.VMEM((NC, 2, half, RC), F32),
            pltpu.VMEM((NC, half, RC), F32),
            pltpu.VMEM((NC, half, RC), F32),
            pltpu.SemaphoreType.DMA((5, NC)),
            pltpu.SemaphoreType.DMA((5, NC)),
            pltpu.SemaphoreType.DMA((NC,)),
        ],
        compiler_params=pltpu.CompilerParams(collective_id=1, has_side_effects=True, vmem_limit_bytes=VMEM_LIMIT),
        name="return_sum",
    )(mine, theirs, hidden, shared_out)


def solution(mesh):
    tok_spec = P(('dp', 'ep'), None)
    expert_spec = P('ep', None, None)

    def local_fn(hidden, norm_gain, w_gate, w1_shared, w3_shared, w2_shared, w1_experts, w3_experts, w2_experts, topk_ids):
        normed = rms_norm(hidden, norm_gain)
        probs = jax.nn.softmax(jnp.dot(normed, w_gate, preferred_element_type=F32), axis=-1)
        chosen = jnp.any(topk_ids[:, :, None] == jnp.arange(EXPERTS), axis=1)
        gate_wts = jnp.where(chosen, ROUTE_SCALE * probs, -1.0).T
        ball, wsb, shared_out = gather_call(normed, gate_wts, w1_shared, w3_shared, w2_shared)
        me = lax.axis_index('ep')
        sel = wsb >= 0.0
        cnt = jnp.sum(sel, axis=2, dtype=jnp.int32)
        before = jnp.arange(SB)[:, None] < jnp.arange(SB)[None, :]
        rank = jnp.einsum('set,tu->seu', sel.astype(BF16), before.astype(BF16), preferred_element_type=F32)
        rank = jnp.where(sel, rank.astype(jnp.int32), -1)
        chip, at = me // 2, jnp.arange(NSB)
        other_x, other_y = at % 2 != chip % 2, at // 2 != chip // 2
        place = jnp.where(other_x, jnp.where(other_y, 2, 1), jnp.where(other_y, 3, 0))
        core = jnp.concatenate([(me % 2)[None], place]).astype(jnp.int32)
        h = up_call(cnt, rank, ball, w1_experts, w3_experts)
        mine, theirs = down_call(cnt, core, rank, wsb, h, w2_experts)
        return return_call(mine, theirs, hidden, shared_out)

    return jax.shard_map(local_fn, mesh=mesh, in_specs=(tok_spec, P(), P(), P(), P(), P(), expert_spec, expert_spec, expert_spec, tok_spec), out_specs=tok_spec, check_vma=False)
```

profile of v0, /device:TPU:0, one launch (start us, length us, event | category | flops | bytes accessed | tf_op | source)
XLA Modules:
  0.0 296.1 jit_solution(9161431156265889474)
XLA Ops:
  0.0 0.0 copy-start
  0.0 0.6 pad_add_fusion.core_ref
  0.6 1.7 fusion
  2.3 0.7 convert_element_type.18
  3.0 0.7 fusion.6
  3.7 1.7 fusion.2.b_any.b_ref
  5.4 0.0 copy-start.2
  5.4 1.0 copy-done.2
  6.5 0.0 copy-done
  6.5 0.5 fusion.8
  7.0 0.6 select_bitcast_fusion.wts_ref
  7.7 54.2 %gather.1 = (bf16[2048,2560]{1,0:T(8,128)(2,1)}, f32[4,8,512]{2,1,0:T(8,128)}, bf16[256,2560]{1,0:T(8,128)(2,1)}) custom-call(bf16[256,2560]{1,0:T(8,128)(2,1)} %copy-done.2, bf16[256,2560]{1,0:T(8,128)(2,1)} %copy-done.2, f32[64,256]{1,0:T(8,128)} %select_bitcast_fusion.wts_ref, bf16[2560,3072]{1,0:T(8,128)(2,1)} %w1.2, bf16[2560,3072]{1,0:T(8,128)(2,1)} %w3.2, ...), custom_call_target="tpu_custom_call" | custom-call | flops 12000000000 | bytes 60000000 | tf_op jit(solution)/shard_map/gather/pallas_call | solution.py:496
  61.9 1.6 convert_reduce_fusion
  63.5 0.8 fusion.3.rank_ref
  64.3 64.5 %up.1.h = bf16[6912,1536]{1,0:T(8,128)(2,1)} custom-call(s32[4,8]{1,0:T(4,128)} %get-tuple-element.15.cnt_ref, s32[4,8,512]{2,1,0:T(8,128)} %fusion.3.rank_ref, bf16[2048,2560]{1,0:T(8,128)(2,1)} %get-tuple-element.11.ball, bf16[8,2560,1536]{2,1,0:T(8,128)(2,1)} %w1.3, bf16[8,2560,1536]{2,1,0:T(8,128)(2,1)} %w3.3), custom_call_target="tpu_custom_call" | custom-call | flops 48000000000 | bytes 140000000 | tf_op jit(solution)/shard_map/up/pallas_call | solution.py:173
  128.8 66.3 %down.1 = (f32[10,4,256,256]{3,2,1,0:T(8,128)}, f32[10,4,256,256]{3,2,1,0:T(8,128)}) custom-call(s32[4,8]{1,0:T(4,128)} %get-tuple-element.15.cnt_ref, s32[5]{0:T(128)} %pad_add_fusion.core_ref, s32[4,8,512]{2,1,0:T(8,128)} %fusion.3.rank_ref, f32[4,8,512]{2,1,0:T(8,128)} %get-tuple-element.10.wt_ref, bf16[6912,1536]{1,0:T(8,128)(2,1)} %up.1.h, ...), custom_call_target="tpu_custom_call" | custom-call | flops 40000000000 | bytes 100000000 | tf_op jit(solution)/shard_map/down/pallas_call | solution.py:358
  195.2 0.0 copy-start.1
  195.2 98.5 %return_sum.1 = bf16[256,2560]{1,0:T(8,128)(2,1)} custom-call(f32[10,4,256,256]{3,2,1,0:T(8,128)} %get-tuple-element.12.mine, f32[10,4,256,256]{3,2,1,0:T(8,128)} %get-tuple-element.13.theirs, bf16[256,2560]{1,0:T(8,128)(2,1)} %y_ref.1, bf16[256,2560]{1,0:T(8,128)(2,1)} %get-tuple-element.14.s_ref), custom_call_target="tpu_custom_call" | custom-call | tf_op jit(solution)/shard_map/return_sum/pallas_call | solution.py:592
  293.7 2.5 copy.13
  296.1 0.0 copy-done.1
  (3 shorter events, 0.1 us)
Async XLA Ops:
  0.0 6.5 %copy-start = (bf16[2560,64]{0,1:T(8,128)(2,1)S(1)}, bf16[2560,64]{0,1:T(8,128)(2,1)}, u32[]{:S(2)}) copy-start(bf16[2560,64]{0,1:T(8,128)(2,1)} %param.12) | copy-start | bytes 983044
  5.4 1.1 copy-start.2
  195.2 101.0 %copy-start.1 = (bf16[2560,64]{0,1:T(8,128)(2,1)S(1)}, bf16[2560,64]{0,1:T(8,128)(2,1)}, u32[]{:S(2)}) copy-start(bf16[2560,64]{0,1:T(8,128)(2,1)} %param.12) | copy-start | bytes 983044
where the time goes:
time: 297 us; the launch traced here: 296 us
  Pallas kernels  284 us (96%)
  other arithmetic  7.65 us (3%)
  local copies, waits for them, and re-layouts  3.52 us (1%)
    pallas_call x1, Pallas kernels, return_call(): pl.pallas_call(return_kernel, out_shape=jax.ShapeDtypeStruct((T, D), BF16...  98.5 us
    pallas_call x1, Pallas kernels, down_call(): pl.pallas_call(down_kernel, out_shape=(out, out), in_specs=[smem, smem, v...  66.3 us
    pallas_call x1, Pallas kernels, up_call(): pl.pallas_call(up_kernel, out_shape=jax.ShapeDtypeStruct((XR, FF), BF16),...  64.5 us
    pallas_call x1, Pallas kernels, gather_call(): pl.pallas_call(gather_kernel, out_shape=(jax.ShapeDtypeStruct((8 * T, D),...  54.2 us

commit v1 on v0

--- a/solution.py
+++ b/solution.py
@@ -28,6 +28,8 @@
 CW = 512
 RC = 256
 NC = D // RC
+KC = 768
+KX = SBR - KC
 VMEM_LIMIT = 66000000
 BF16 = jnp.bfloat16
 F32 = jnp.float32
@@ -199,8 +201,8 @@
     )(cnt, rank, ball, w1, w3)
 
 
-def down_kernel(cnt_ref, core_ref, rank_ref, wt_ref, h, w2, mine, theirs,
-                hs, ebuf, kbuf, pbuf, wbuf, abuf, wsplit, ng, eoff, est, boff, nsb_g, hsem, wsem, osem):
+def down_kernel(cnt_ref, core_ref, rank_ref, wt_ref, h, w2, eblk, mine, theirs,
+                hs, ebuf, kbuf, pbuf, wbuf, abuf, wsplit, ng, eoff, est, boff, nsb_g, hsem, wsem, osem, ksem):
     steps = (D // CW) * NE
 
     def w_copy(st, slot):
@@ -225,41 +227,48 @@
         return 0
 
     lax.fori_loop(0, nh, h_start, 0)
-    for s in range(NSB):
-        w = wt_ref[s]
-        hi = w.astype(BF16).astype(F32)
-        mid = (w - hi).astype(BF16).astype(F32)
-        wsplit[0, s] = hi
-        wsplit[1, s] = mid
-        wsplit[2, s] = w - hi - mid
-    rows16 = lax.broadcasted_iota(jnp.int32, (G, SB), 0)
-    for s in range(NSB):
-        for e in range(NE):
-            rk = jnp.broadcast_to(rank_ref[s, e:e + 1, :], (G, SB))
-            parts = [jnp.broadcast_to(wsplit[i, s, e:e + 1, :], (G, SB)) for i in range(3)]
-
-            def build(g, _, s=s, e=e, rk=rk, parts=parts):
-                row = pl.multiple_of((boff[s * NE + e] + g) * G, G)
-                hit = rk == rows16 + g * G
-                for i in range(3):
-                    pbuf[s, i, pl.ds(row, G), :] = jnp.where(hit, parts[i], 0.0).astype(BF16)
+    most = jnp.maximum(jnp.maximum(nsb_g[0], nsb_g[1]), jnp.maximum(nsb_g[2], nsb_g[3]))
+    over = most > KC // G
+
+    @pl.when(over)
+    def _():
+        rows16 = lax.broadcasted_iota(jnp.int32, (G, SB), 0)
+        pbuf[...] = jnp.zeros_like(pbuf)
+        for s in range(NSB):
+            w = wt_ref[s]
+            hi = w.astype(BF16).astype(F32)
+            mid = (w - hi).astype(BF16).astype(F32)
+            wsplit[0, s] = hi
+            wsplit[1, s] = mid
+            wsplit[2, s] = w - hi - mid
+
+        def segment(q, _):
+            s, e = q // NE, q % NE
+            rk = jnp.broadcast_to(rank_ref[s, pl.ds(e, 1), :], (G, SB))
+            parts = [jnp.broadcast_to(wsplit[i, s, pl.ds(e, 1), :], (G, SB)) for i in range(3)]
+
+            def build(g, _):
+                k = boff[q] + g
+
+                @pl.when(k >= KC // G)
+                def _():
+                    row = pl.multiple_of((k - KC // G) * G, G)
+                    hit = rk == rows16 + g * G
+                    for i in range(3):
+                        pbuf[s, i, pl.ds(row, G), :] = jnp.where(hit, parts[i], 0.0).astype(BF16)
+
                 return 0
 
-            lax.fori_loop(0, ng[s * NE + e], build, 0)
-
-        def clear(g, _, s=s):
-            row = pl.multiple_of(g * G, G)
-            for i in range(3):
-                pbuf[s, i, pl.ds(row, G), :] = jnp.zeros((G, SB), BF16)
-            return 0
-
-        lax.fori_loop(nsb_g[s], -(-nsb_g[s] // (TM // G)) * (TM // G), clear, 0)
+            return lax.fori_loop(0, ng[q], build, 0)
+
+        lax.fori_loop(0, NSB * NE, segment, 0)
+
     kbuf[...] = jnp.zeros_like(kbuf)
     lax.fori_loop(0, nh, h_wait, 0)
 
     core = core_ref[0]
 
-    def out_copies(c, s, slot):
+    def out_copies(c, s):
         rel = core_ref[1 + s]
         keep = pl.multiple_of(core * 256, 256)
         give = pl.multiple_of(256 - core * 256, 256)
@@ -267,9 +276,12 @@
         for i in range(CW // RC):
             cols = pl.ds(i * RC, RC)
             j = c * (CW // RC) + i
-            out.append(pltpu.make_async_copy(abuf.at[slot, pl.ds(give, 256), cols], theirs.at[j, rel], osem.at[slot, i, 0]))
-            out.append(pltpu.make_async_copy(abuf.at[slot, pl.ds(keep, 256), cols], mine.at[j, rel], osem.at[slot, i, 1]))
+            out.append(pltpu.make_async_copy(abuf.at[pl.ds(give, 256), cols], theirs.at[j, rel], osem.at[i, 0]))
+            out.append(pltpu.make_async_copy(abuf.at[pl.ds(keep, 256), cols], mine.at[j, rel], osem.at[i, 1]))
         return out
+
+    def k_copies(c, s, slot):
+        return [pltpu.make_async_copy(kbuf.at[slot, pl.ds(0, KC), pl.ds(i * RC, RC)], eblk.at[c * (CW // RC) + i, s], ksem.at[slot, i]) for i in range(CW // RC)]
 
     def column(c, _):
         def expert(e, _):
@@ -307,46 +319,49 @@
         def block(s, _):
             slot = s % 2
 
+            @pl.when(c * NSB + s >= 2)
+            def _():
+                for cp in k_copies(c, s, slot):
+                    cp.wait()
+
             def segment(e, _):
                 def move(g, _):
                     row = pl.multiple_of((boff[s * NE + e] + g) * G, G)
                     src = pl.multiple_of((eoff[s * NE + e] + g) * G, G)
-                    kbuf[pl.ds(row, G), :] = ebuf[pl.ds(src, G), :]
+                    kbuf[slot, pl.ds(row, G), :] = ebuf[pl.ds(src, G), :]
                     return 0
 
                 return lax.fori_loop(0, ng[s * NE + e], move, 0)
 
             lax.fori_loop(0, NE, segment, 0)
-            nk = (nsb_g[s] + TM // G - 1) // (TM // G)
-
-            @pl.when(c * NSB + s >= 2)
+            for cp in k_copies(c, s, slot):
+                cp.start()
+
+            @pl.when(over)
             def _():
-                for cp in out_copies(c, s, slot):
+                nk = (nsb_g[s] + TM // G - 1) // (TM // G)
+                abuf[...] = jnp.zeros_like(abuf)
+
+                def tile(kt, _):
+                    ek = kbuf[slot, pl.ds(pl.multiple_of(kt * TM, TM), TM), :]
+                    rows = pl.ds(pl.multiple_of(kt * TM - KC, TM), TM)
+                    for i in range(3):
+                        abuf[...] += lax.dot_general(pbuf[s, i, rows, :], ek, (((0,), (0,)), ((), ())), preferred_element_type=F32)
+                    return 0
+
+                lax.fori_loop(KC // TM, nk, tile, 0)
+                for cp in out_copies(c, s):
+                    cp.start()
+                for cp in out_copies(c, s):
                     cp.wait()
 
-            abuf[slot] = jnp.zeros((SB, CW), F32)
-
-            def tile(kt, _):
-                rows = pl.ds(pl.multiple_of(kt * TM, TM), TM)
-                ek = kbuf[rows, :]
-                for half in range(2):
-                    toks = slice(half * 256, half * 256 + 256)
-                    tot = abuf[slot, toks, :]
-                    for i in range(3):
-                        tot = tot + lax.dot_general(pbuf[s, i, rows, toks], ek, (((0,), (0,)), ((), ())), preferred_element_type=F32)
-                    abuf[slot, toks, :] = tot
-                return 0
-
-            lax.fori_loop(0, nk, tile, 0)
-            for cp in out_copies(c, s, slot):
-                cp.start()
             return 0
 
         return lax.fori_loop(0, NSB, block, 0)
 
     lax.fori_loop(0, D // CW, column, 0)
     for s in (NSB - 2, NSB - 1):
-        for cp in out_copies(D // CW - 1, s, s % 2):
+        for cp in k_copies(D // CW - 1, s, s % 2):
             cp.wait()
 
 
@@ -357,16 +372,16 @@
     out = jax.ShapeDtypeStruct((NC, NSB, 256, RC), F32)
     return pl.pallas_call(
         down_kernel,
-        out_shape=(out, out),
+        out_shape=(jax.ShapeDtypeStruct((NC, NSB, KC, RC), BF16), out, out),
         in_specs=[smem, smem, vmem, vmem, any_spec, any_spec],
-        out_specs=(any_spec, any_spec),
+        out_specs=(any_spec, any_spec, any_spec),
         scratch_shapes=[
             pltpu.VMEM((XR, FF), BF16),
             pltpu.VMEM((XR, CW), BF16),
-            pltpu.VMEM((SBR, CW), BF16),
-            pltpu.VMEM((NSB, 3, SBR, SB), BF16),
+            pltpu.VMEM((2, SBR, CW), BF16),
+            pltpu.VMEM((NSB, 3, KX, SB), BF16),
             pltpu.VMEM((3, FF, CW), BF16),
-            pltpu.VMEM((2, SB, CW), F32),
+            pltpu.VMEM((SB, CW), F32),
             pltpu.VMEM((3, NSB, NE, SB), F32),
             pltpu.SMEM((NSB * NE,), jnp.int32),
             pltpu.SMEM((NSB * NE,), jnp.int32),
@@ -375,7 +390,8 @@
             pltpu.SMEM((NSB,), jnp.int32),
             pltpu.SemaphoreType.DMA((1,)),
             pltpu.SemaphoreType.DMA((3,)),
-            pltpu.SemaphoreType.DMA((2, CW // RC, 2)),
+            pltpu.SemaphoreType.DMA((CW // RC, 2)),
+            pltpu.SemaphoreType.DMA((2, CW // RC)),
         ],
         compiler_params=pltpu.CompilerParams(vmem_limit_bytes=VMEM_LIMIT),
         cost_estimate=pl.CostEstimate(flops=40_000_000_000, bytes_accessed=100_000_000, transcendentals=0),
@@ -402,7 +418,7 @@
     pl.semaphore_wait(barrier, len(others))
 
 
-def gather_kernel(b_any, b_ref, wts_ref, w1, w3, w2, ball, wall, s_ref, w13buf, w2buf, acc, send, recv, wsend, wrecv, local, wsem):
+def gather_kernel(b_any, b_ref, wts_ref, w1, w3, w2, ball, wall_out, rank_ref, cnt_ref, pt, s_ref, wall, ptbuf, cols_buf, w13buf, w2buf, acc, send, recv, wsend, wrecv, local, wsem, psem):
     me, pn, xn, yn = neighbours()
     diag = xn + yn - me
     half = T // 2
@@ -475,6 +491,53 @@
     third = [relay(10, xn, 1, pn), relay(11, yn, 0, pn)]
     for c in third:
         c.start()
+    for c in small:
+        c.wait_recv()
+    keep[1].wait()
+    before = jnp.where(lax.broadcasted_iota(jnp.int32, (SB, SB), 0) < lax.broadcasted_iota(jnp.int32, (SB, SB), 1), 1.0, 0.0).astype(BF16)
+    row = lax.broadcasted_iota(jnp.int32, (1, KC), 1)
+    puts = []
+    for s in range(NSB):
+        slot = s % 2
+        w = wall[s]
+        wall_out[s] = w
+        sel = jnp.where(w >= 0.0, 1.0, 0.0)
+        rank = jnp.where(w >= 0.0, jnp.dot(sel.astype(BF16), before, preferred_element_type=F32), -1.0)
+        rank_ref[s] = rank.astype(jnp.int32)
+        count = jnp.sum(sel, axis=1, keepdims=True).astype(jnp.int32)
+        cnt_ref[s] = jnp.broadcast_to(count, (NE, 128))
+        wide = jnp.broadcast_to(count, (NE, KC))
+        start = jnp.zeros((1, KC), jnp.int32)
+        local_row = []
+        for e in range(NE):
+            n = wide[e:e + 1]
+            at = row - start
+            local_row.append(jnp.where((at >= 0) & (at < n), at, -2).astype(F32))
+            start = start + (n + (G - 1)) // G * G
+        pad = jnp.zeros((128 - NE, SB), F32)
+        cols_buf[0] = jnp.concatenate([rank, pad], axis=0).T
+        cols_buf[1] = jnp.concatenate([w, pad], axis=0).T
+        if s >= 2:
+            puts[s - 2].wait()
+
+        def fill(tb, _, slot=slot, local_row=local_row):
+            toks = pl.ds(pl.multiple_of(tb * 32, 32), 32)
+            rk = cols_buf[0, toks, :]
+            wt = cols_buf[1, toks, :]
+            total = jnp.zeros((32, KC), F32)
+            for e in range(NE):
+                total = jnp.where(rk[:, e:e + 1] == local_row[e], wt[:, e:e + 1], total)
+            hi = total.astype(BF16)
+            rest = total - hi.astype(F32)
+            mid = rest.astype(BF16)
+            ptbuf[slot, 0, toks, :] = hi
+            ptbuf[slot, 1, toks, :] = mid
+            ptbuf[slot, 2, toks, :] = (rest - mid.astype(F32)).astype(BF16)
+            return 0
+
+        lax.fori_loop(0, SB // 32, fill, 0)
+        puts.append(pltpu.make_async_copy(ptbuf.at[slot], pt.at[s], psem.at[slot]))
+        puts[s].start()
     second[0].wait_recv()
     second[1].wait_recv()
     fourth = [relay(12, diag, 0, pn), relay(13, diag, 1, pn)]
@@ -485,9 +548,10 @@
     for c in (*first, *second, *third, *fourth):
         c.wait_send()
     for c in small:
-        c.wait()
-    for c in keep:
-        c.wait()
+        c.wait_send()
+    keep[0].wait()
+    puts[2].wait()
+    puts[3].wait()
 
 
 def gather_call(b, wts, w1, w3, w2):
@@ -495,10 +559,20 @@
     vmem = pl.BlockSpec(memory_space=pltpu.VMEM)
     return pl.pallas_call(
         gather_kernel,
-        out_shape=(jax.ShapeDtypeStruct((8 * T, D), BF16), jax.ShapeDtypeStruct((NSB, NE, SB), F32), jax.ShapeDtypeStruct((T, D), BF16)),
+        out_shape=(
+            jax.ShapeDtypeStruct((8 * T, D), BF16),
+            jax.ShapeDtypeStruct((NSB, NE, SB), F32),
+            jax.ShapeDtypeStruct((NSB, NE, SB), jnp.int32),
+            jax.ShapeDtypeStruct((NSB, NE, 128), jnp.int32),
+            jax.ShapeDtypeStruct((NSB, 3, SB, KC), BF16),
+            jax.ShapeDtypeStruct((T, D), BF16),
+        ),
         in_specs=[any_spec, vmem, vmem, any_spec, any_spec, any_spec],
-        out_specs=(any_spec, any_spec, vmem),
+        out_specs=(any_spec, vmem, vmem, vmem, any_spec, vmem),
         scratch_shapes=[
+            pltpu.VMEM((NSB, NE, SB), F32),
+            pltpu.VMEM((2, 3, SB, KC), BF16),
+            pltpu.VMEM((2, SB, 128), F32),
             pltpu.VMEM((3, 2, D, SF), BF16),
             pltpu.VMEM((3, SF, D), BF16),
             pltpu.VMEM((T, D), F32),
@@ -508,6 +582,7 @@
             pltpu.SemaphoreType.DMA((7,)),
             pltpu.SemaphoreType.DMA((2,)),
             pltpu.SemaphoreType.DMA((3, 3)),
+            pltpu.SemaphoreType.DMA((2,)),
         ],
         compiler_params=pltpu.CompilerParams(collective_id=0, has_side_effects=True, vmem_limit_bytes=VMEM_LIMIT),
         cost_estimate=pl.CostEstimate(flops=12_000_000_000, bytes_accessed=60_000_000, transcendentals=0),
@@ -515,16 +590,19 @@
     )(b, b, wts, w1, w3, w2)
 
 
-def return_kernel(mine, theirs, y_ref, s_ref, out_ref, own, r1, r2x, r2y, r3x, r3y, send, recv, load):
+def return_kernel(cnt_ref, pt, eblk, mine, theirs, y_ref, s_ref, out_ref, ptv, ev, own, give, r1, r2x, r2y, r3x, r3y, send, recv, load, esem, psem):
     me, pn, xn, yn = neighbours()
     half = T // 2
     top, low = pl.ds(0, half), pl.ds(half, half)
 
     def load_of(j):
-        return pltpu.make_async_copy(mine.at[j], own.at[j], load.at[j])
+        return (pltpu.make_async_copy(theirs.at[j], give.at[j], load.at[0, j]), pltpu.make_async_copy(mine.at[j], own.at[j], load.at[1, j]))
+
+    def e_of(j, slot):
+        return pltpu.make_async_copy(eblk.at[j], ev.at[slot], esem.at[slot])
 
     def core_of(j):
-        return remote(theirs.at[j], r1.at[j], send.at[0, j], recv.at[0, j], pn)
+        return remote(give.at[j], r1.at[j], send.at[0, j], recv.at[0, j], pn)
 
     def x_of(j):
         return remote(own.at[j, pl.ds(1, 2), top, :], r2x.at[j], send.at[1, j], recv.at[1, j], xn)
@@ -545,12 +623,44 @@
 
         lax.fori_loop(0, NC, run, 0)
 
+    rows_over = jnp.int32(0)
+    for s in range(NSB):
+        n = jnp.int32(0)
+        for e in range(NE):
+            n = n + (cnt_ref[s, e] + (G - 1)) // G
+        rows_over = jnp.maximum(rows_over, n - KC // G)
+    over = jnp.full((T, RC), rows_over, jnp.int32) > 0
+
     def begin(j):
-        load_of(j).start()
+        for c in load_of(j):
+            c.start()
+
+    def add_up(j, buf, first_tok):
+        slot = lax.rem(j, 2)
+        toks = pl.ds(pl.multiple_of(first_tok, T), T)
+
+        def block(s, _):
+            dx = lax.rem(lax.rem(s, 2) + lax.rem(me // 2, 2), 2)
+            dy = lax.rem(s // 2 + me // 4, 2)
+            place = dx + 3 * dy - 2 * dx * dy
+            total = jnp.where(over, buf[j, place], 0.0)
+            ek = ev[slot, s]
+            for i in range(3):
+                total = total + jnp.dot(ptv[s, i, toks, :], ek, preferred_element_type=F32)
+            buf[j, place] = total
+            return 0
+
+        lax.fori_loop(0, NSB, block, 0)
+
+    def make(j):
+        e_of(j, lax.rem(j, 2)).wait()
+        for c in load_of(j):
+            c.wait()
+        add_up(j, give, T - lax.rem(me, 2) * T)
         core_of(j).start()
+        add_up(j, own, lax.rem(me, 2) * T)
 
     def pair(j):
-        load_of(j).wait()
         core_of(j).wait_recv()
         own[j, 1:] = own[j, 1:] + r1[j, 1:]
         x_of(j).start()
@@ -577,24 +687,45 @@
         for c in (core_of(j), x_of(j), y_of(j), y_last(j), x_last(j)):
             c.wait_send()
 
+    e_of(0, 0).start()
+    pt_copies = [pltpu.make_async_copy(pt.at[s], ptv.at[s], psem.at[s]) for s in range(NSB)]
+    for c in pt_copies:
+        c.start()
+    e_of(1, 1).start()
     enter([pn, xn, yn])
     each(begin)
-    each(pair)
+    for c in pt_copies:
+        c.wait()
+
+    def steady(j, _):
+        make(j)
+
+        @pl.when(j + 2 < NC)
+        def _():
+            e_of(j + 2, lax.rem(j, 2)).start()
+
+        pair(j)
+        return 0
+
+    lax.fori_loop(0, NC, steady, 0)
     each(onward)
     each(finish)
     each(drain)
 
 
-def return_call(mine, theirs, hidden, shared_out):
+def return_call(cnt, pt, eblk, mine, theirs, hidden, shared_out):
     any_spec = pl.BlockSpec(memory_space=pl.ANY)
     vmem = pl.BlockSpec(memory_space=pltpu.VMEM)
     half = T // 2
     return pl.pallas_call(
         return_kernel,
         out_shape=jax.ShapeDtypeStruct((T, D), BF16),
-        in_specs=[any_spec, any_spec, vmem, vmem],
+        in_specs=[pl.BlockSpec(memory_space=pltpu.SMEM), any_spec, any_spec, any_spec, any_spec, vmem, vmem],
         out_specs=vmem,
         scratch_shapes=[
+            pltpu.VMEM((NSB, 3, SB, KC), BF16),
+            pltpu.VMEM((2, NSB, KC, RC), BF16),
+            pltpu.VMEM((NC, NSB, T, RC), F32),
             pltpu.VMEM((NC, NSB, T, RC), F32),
             pltpu.VMEM((NC, NSB, T, RC), F32),
             pltpu.VMEM((NC, 2, half, RC), F32),
@@ -603,11 +734,13 @@
             pltpu.VMEM((NC, half, RC), F32),
             pltpu.SemaphoreType.DMA((5, NC)),
             pltpu.SemaphoreType.DMA((5, NC)),
-            pltpu.SemaphoreType.DMA((NC,)),
+            pltpu.SemaphoreType.DMA((2, NC)),
+            pltpu.SemaphoreType.DMA((2,)),
+            pltpu.SemaphoreType.DMA((NSB,)),
         ],
         compiler_params=pltpu.CompilerParams(collective_id=1, has_side_effects=True, vmem_limit_bytes=VMEM_LIMIT),
         name="return_sum",
-    )(mine, theirs, hidden, shared_out)
+    )(cnt, pt, eblk, mine, theirs, hidden, shared_out)
 
 
 def solution(mesh):
@@ -619,19 +752,15 @@
         probs = jax.nn.softmax(jnp.dot(normed, w_gate, preferred_element_type=F32), axis=-1)
         chosen = jnp.any(topk_ids[:, :, None] == jnp.arange(EXPERTS), axis=1)
         gate_wts = jnp.where(chosen, ROUTE_SCALE * probs, -1.0).T
-        ball, wsb, shared_out = gather_call(normed, gate_wts, w1_shared, w3_shared, w2_shared)
+        ball, wsb, rank, counts, pt, shared_out = gather_call(normed, gate_wts, w1_shared, w3_shared, w2_shared)
+        cnt = counts[:, :, 0]
         me = lax.axis_index('ep')
-        sel = wsb >= 0.0
-        cnt = jnp.sum(sel, axis=2, dtype=jnp.int32)
-        before = jnp.arange(SB)[:, None] < jnp.arange(SB)[None, :]
-        rank = jnp.einsum('set,tu->seu', sel.astype(BF16), before.astype(BF16), preferred_element_type=F32)
-        rank = jnp.where(sel, rank.astype(jnp.int32), -1)
         chip, at = me // 2, jnp.arange(NSB)
         other_x, other_y = at % 2 != chip % 2, at // 2 != chip // 2
         place = jnp.where(other_x, jnp.where(other_y, 2, 1), jnp.where(other_y, 3, 0))
         core = jnp.concatenate([(me % 2)[None], place]).astype(jnp.int32)
         h = up_call(cnt, rank, ball, w1_experts, w3_experts)
-        mine, theirs = down_call(cnt, core, rank, wsb, h, w2_experts)
-        return return_call(mine, theirs, hidden, shared_out)
+        eblk, mine, theirs = down_call(cnt, core, rank, wsb, h, w2_experts)
+        return return_call(cnt, pt, eblk, mine, theirs, hidden, shared_out)
 
     return jax.shard_map(local_fn, mesh=mesh, in_specs=(tok_spec, P(), P(), P(), P(), P(), expert_spec, expert_spec, expert_spec, tok_spec), out_specs=tok_spec, check_vma=False)

time: 297 us -> 277 us (0.933)
  Pallas kernels: 284 us -> 265 us
    pallas_call x1, Pallas kernels: 66.3 us -> 43.5 us  [down_call(): pl.pallas_call(down_kernel, out_shape=(jax.ShapeDtypeStruct((NC, NSB, KC,...]
where the time goes in v1:
time: 277 us; the launch traced here: 276 us
  Pallas kernels  265 us (96%)
  other arithmetic  6.1 us (2%)
  local copies, waits for them, and re-layouts  4.96 us (2%)
    pallas_call x1, Pallas kernels, return_call(): pl.pallas_call(return_kernel, out_shape=jax.ShapeDtypeStruct((T, D), BF16...  101 us
    pallas_call x1, Pallas kernels, up_call(): pl.pallas_call(up_kernel, out_shape=jax.ShapeDtypeStruct((XR, FF), BF16),...  66 us
    pallas_call x1, Pallas kernels, gather_call(): pl.pallas_call(gather_kernel, out_shape=(jax.ShapeDtypeStruct((8 * T, D),...  54.3 us
    pallas_call x1, Pallas kernels, down_call(): pl.pallas_call(down_kernel, out_shape=(jax.ShapeDtypeStruct((NC, NSB, KC,...  43.5 us

profile of v1, /device:TPU:0, one launch (start us, length us, event | category | flops | bytes accessed | tf_op | source)
XLA Modules:
  0.0 276.3 jit_solution(8613449139870358241)
XLA Ops:
  0.0 0.0 copy-start
  0.0 0.6 pad_add_fusion.core_ref
  0.6 1.7 fusion
  2.3 0.7 convert_element_type.10
  3.0 0.7 fusion.3
  3.7 1.7 fusion.2.b_any.b_ref
  5.4 0.0 copy-start.2
  5.4 1.0 copy-done.2
  6.5 0.0 copy-done
  6.5 0.5 fusion.5
  7.1 0.6 select_bitcast_fusion.wts_ref
  7.7 54.3 %gather.1 = (bf16[2048,2560]{1,0:T(8,128)(2,1)}, f32[4,8,512]{2,1,0:T(8,128)}, s32[4,8,512]{2,1,0:T(8,128)}, s32[4,8,128]{2,1,0:T(8,128)}, bf16[4,3,512,768]{3,2,1,0:T(8,128)(2,1)}, /*index=5*/bf16[256,2560]{1,0:T(8,128)(2,1)}) custom-call(bf16[256,2560]{1,0:T(8,128)(2,1)} %copy-done.2, bf16[256,2560]{1,0:T(8,128)(2,1)} %copy-done.2, ...), custom_call_target="tpu_custom_call" | custom-call | flops 12000000000 | bytes 60000000 | tf_op jit(solution)/shard_map/gather/pallas_call | solution.py:560
  62.0 1.4 slice_reduce_fusion.cnt_ref
  63.5 66.0 %up.1.h = bf16[6912,1536]{1,0:T(8,128)(2,1)} custom-call(s32[4,8]{1,0:T(4,128)} %slice_reduce_fusion.cnt_ref, s32[4,8,512]{2,1,0:T(8,128)} %get-tuple-element.16.rank_ref, bf16[2048,2560]{1,0:T(8,128)(2,1)} %get-tuple-element.18.ball, bf16[8,2560,1536]{2,1,0:T(8,128)(2,1)} %w1.3, bf16[8,2560,1536]{2,1,0:T(8,128)(2,1)} %w3.3), custom_call_target="tpu_custom_call" | custom-call | flops 48000000000 | bytes 140000000 | tf_op jit(solution)/shard_map/up/pallas_call | solution.py:175
  129.5 43.5 %down.1 = (bf16[10,4,768,256]{3,2,1,0:T(8,128)(2,1)}, f32[10,4,256,256]{3,2,1,0:T(8,128)}, f32[10,4,256,256]{3,2,1,0:T(8,128)}) custom-call(s32[4,8]{1,0:T(4,128)} %slice_reduce_fusion.cnt_ref, s32[5]{0:T(128)} %pad_add_fusion.core_ref, s32[4,8,512]{2,1,0:T(8,128)} %get-tuple-element.16.rank_ref, f32[4,8,512]{2,1,0:T(8,128)} %get-tuple-element.17.wt_ref, ...), custom_call_target="tpu_custom_call" | custom-call | flops 40000000000 | bytes 100000000 | tf_op jit(solution)/shard_map/down/pallas_call | solution.py:373
  173.0 0.0 copy-start.1
  173.0 100.9 %return_sum.1 = bf16[256,2560]{1,0:T(8,128)(2,1)} custom-call(s32[4,8]{1,0:T(4,128)} %slice_reduce_fusion.cnt_ref, bf16[4,3,512,768]{3,2,1,0:T(8,128)(2,1)} %get-tuple-element.15.pt, bf16[10,4,768,256]{3,2,1,0:T(8,128)(2,1)} %get-tuple-element.19.eblk, f32[10,4,256,256]{3,2,1,0:T(8,128)} %get-tuple-element.20.mine, ...), custom_call_target="tpu_custom_call" | custom-call | tf_op jit(solution)/shard_map/return_sum/pallas_call | solution.py:720
  273.8 2.5 copy.14
  276.3 0.0 copy-done.1
  (3 shorter events, 0.1 us)
Async XLA Ops:
  0.0 6.5 %copy-start = (bf16[2560,64]{0,1:T(8,128)(2,1)S(1)}, bf16[2560,64]{0,1:T(8,128)(2,1)}, u32[]{:S(2)}) copy-start(bf16[2560,64]{0,1:T(8,128)(2,1)} %param.12) | copy-start | bytes 983044
  5.4 1.1 copy-start.2
  173.0 103.3 %copy-start.1 = (bf16[2560,64]{0,1:T(8,128)(2,1)S(1)}, bf16[2560,64]{0,1:T(8,128)(2,1)}, u32[]{:S(2)}) copy-start(bf16[2560,64]{0,1:T(8,128)(2,1)} %param.12) | copy-start | bytes 983044

commit v2 on v1

--- a/solution.py
+++ b/solution.py
@@ -22,6 +22,7 @@
 SBR = 1792
 FC = 512
 NF = FF // FC
+DH = D // 2
 T = 256
 SHARED = 3072
 SF = 256
@@ -67,21 +68,18 @@
         return (pltpu.make_async_copy(w1.at[e, :, cols], wbuf.at[slot, 0], wsem.at[slot, 0]),
                 pltpu.make_async_copy(w3.at[e, :, cols], wbuf.at[slot, 1], wsem.at[slot, 1]))
 
-    def b_copy(s, slot):
-        return pltpu.make_async_copy(ball.at[pl.ds(s * SB, SB), :], bbuf.at[slot], bsem.at[slot])
+    def b_copy(s, half):
+        return pltpu.make_async_copy(ball.at[pl.ds(s * SB, SB), pl.ds(half * DH, DH)], bbuf.at[half], bsem.at[half])
 
     b_copy(0, 0).start()
-    for c in w_copies(0, 0):
-        c.start()
-    for c in w_copies(1, 1):
-        c.start()
+    b_copy(0, 1).start()
+    for st in range(3):
+        for c in w_copies(st, st):
+            c.start()
     offsets(cnt_ref, ng, eoff, est, boff, nsb_g)
     rows16 = lax.broadcasted_iota(jnp.int32, (G, SB), 0)
 
     for s in range(NSB):
-        slot = s % 2
-        if s + 1 < NSB:
-            b_copy(s + 1, 1 - slot).start()
         for e in range(NE):
             rk = jnp.broadcast_to(rank_ref[s, e:e + 1, :], (G, SB))
 
@@ -93,23 +91,26 @@
                 return 0
 
             lax.fori_loop(0, ng[s * NE + e], build, 0)
-        b_copy(s, slot).wait()
-
-        def tile(m, _, s=s, slot=slot):
-            prow = pbuf[pl.ds(pl.multiple_of(m * TM, TM), TM), :]
-            for n in range(D // 512):
-                cols = slice(n * 512, (n + 1) * 512)
-                tbuf[:, cols] = jnp.dot(prow, bbuf[slot, :, cols], preferred_element_type=F32).astype(BF16)
-
-            def put(j, _):
-                row = pl.multiple_of(dst[m * (TM // G) + j] * G, G)
-                xs[pl.ds(row, G), :] = tbuf[pl.ds(pl.multiple_of(j * G, G), G), :]
+        for half in range(2):
+            b_copy(s, half).wait()
+
+            def tile(m, _, s=s, half=half):
+                prow = pbuf[pl.ds(pl.multiple_of(m * TM, TM), TM), :]
+                for n in range(5):
+                    cols = slice(n * 256, (n + 1) * 256)
+                    tbuf[:, cols] = jnp.dot(prow, bbuf[half, :, cols], preferred_element_type=F32).astype(BF16)
+
+                def put(j, _):
+                    row = pl.multiple_of(dst[m * (TM // G) + j] * G, G)
+                    xs[pl.ds(row, G), half * DH:(half + 1) * DH] = tbuf[pl.ds(pl.multiple_of(j * G, G), G), :]
+                    return 0
+
+                lax.fori_loop(0, jnp.minimum(TM // G, nsb_g[s] - m * (TM // G)), put, 0)
                 return 0
 
-            lax.fori_loop(0, jnp.minimum(TM // G, nsb_g[s] - m * (TM // G)), put, 0)
-            return 0
-
-        lax.fori_loop(0, (nsb_g[s] + TM // G - 1) // (TM // G), tile, 0)
+            lax.fori_loop(0, (nsb_g[s] + TM // G - 1) // (TM // G), tile, 0)
+            if s + 1 < NSB:
+                b_copy(s + 1, half).start()
 
     def h_copy(hs, row, col, size):
         return pltpu.make_async_copy(hbuf.at[hs, pl.ds(0, size), :], h_out.at[pl.ds(row, size), pl.ds(col, FC)], hsem.at[0])
@@ -121,7 +122,7 @@
                 h_copy(0, 0, 0, q * 64).wait()
 
     def step(st, k):
-        slot = st % 2
+        slot = lax.rem(st, 3)
         e = st // NF
         col = pl.multiple_of((st % NF) * FC, FC)
         for c in w_copies(st, slot):
@@ -132,10 +133,12 @@
         def work(row, size, k):
             row = pl.multiple_of(row, G)
             hs = k % 2
-            x = xs[pl.ds(row, size), :]
-            gate = jnp.dot(x, wbuf[slot, 0], preferred_element_type=F32)
-            lin = jnp.dot(x, wbuf[slot, 1], preferred_element_type=F32)
-            hbuf[hs, pl.ds(0, size), :] = (jax.nn.silu(gate) * lin).astype(BF16)
+            for n in range(FC // 256):
+                cols = slice(n * 256, (n + 1) * 256)
+                x = xs[pl.ds(row, size), :]
+                gate = jnp.dot(x, wbuf[slot, 0, :, cols], preferred_element_type=F32)
+                lin = jnp.dot(x, wbuf[slot, 1, :, cols], preferred_element_type=F32)
+                hbuf[hs, pl.ds(0, size), cols] = (jax.nn.silu(gate) * lin).astype(BF16)
 
             @pl.when(k > 0)
             def _():
@@ -158,9 +161,9 @@
             def _(size=size):
                 work(at, size, k)
 
-        @pl.when(st + 2 < NE * NF)
+        @pl.when(st + 3 < NE * NF)
         def _():
-            for c in w_copies(st + 2, slot):
+            for c in w_copies(st + 3, slot):
                 c.start()
 
         return k + jnp.where(rem > 0, 1, 0)
@@ -179,10 +182,10 @@
         out_specs=any_spec,
         scratch_shapes=[
             pltpu.VMEM((XR, D), BF16),
-            pltpu.VMEM((2, SB, D), BF16),
+            pltpu.VMEM((2, SB, DH), BF16),
             pltpu.VMEM((SBR, SB), BF16),
-            pltpu.VMEM((TM, D), BF16),
-            pltpu.VMEM((2, 2, D, FC), BF16),
+            pltpu.VMEM((TM, DH), BF16),
+            pltpu.VMEM((3, 2, D, FC), BF16),
             pltpu.VMEM((2, TM, FC), BF16),
             pltpu.SMEM((NSB * NE,), jnp.int32),
             pltpu.SMEM((NSB * NE,), jnp.int32),
@@ -192,7 +195,7 @@
             pltpu.SMEM((SBR // G,), jnp.int32),
             pltpu.SMEM((1,), jnp.int32),
             pltpu.SemaphoreType.DMA((2,)),
-            pltpu.SemaphoreType.DMA((2, 2)),
+            pltpu.SemaphoreType.DMA((3, 2)),
             pltpu.SemaphoreType.DMA((1,)),
         ],
         compiler_params=pltpu.CompilerParams(vmem_limit_bytes=VMEM_LIMIT),
@@ -201,34 +204,128 @@
     )(cnt, rank, ball, w1, w3)
 
 
-def down_kernel(cnt_ref, core_ref, rank_ref, wt_ref, h, w2, eblk, mine, theirs,
-                hs, ebuf, kbuf, pbuf, wbuf, abuf, wsplit, ng, eoff, est, boff, nsb_g, hsem, wsem, osem, ksem):
-    steps = (D // CW) * NE
-
-    def w_copy(st, slot):
-        col = pl.multiple_of((st // NE) * CW, CW)
-        return pltpu.make_async_copy(w2.at[st % NE, :, pl.ds(col, CW)], wbuf.at[slot], wsem.at[slot])
-
-    def h_copy(t):
-        rows = pl.ds(pl.multiple_of(t * TM, TM), TM)
-        return pltpu.make_async_copy(h.at[rows, :], hs.at[rows, :], hsem.at[0])
-
-    for st in range(3):
-        w_copy(st, st).start()
+def down_kernel(cnt_ref, core_ref, rank_ref, wt_ref, h, w2, eblk, eover, mine, theirs,
+                hs, wbuf, tbuf, zbuf, kbuf, pbuf, abuf, wsplit, ng, eoff, est, boff, nsb_g, gdst, trow, tnum, hsem, wsem, gsem, zsem, osem, ksem):
+    def w_copy(e, slot):
+        return pltpu.make_async_copy(w2.at[e], wbuf.at[slot], wsem.at[slot])
+
+    def h_copy(t, slot):
+        return pltpu.make_async_copy(h.at[pl.ds(pl.multiple_of(trow[t] * G, G), TM), :], hs.at[slot], hsem.at[slot])
+
+    def z_copy(s, k):
+        return pltpu.make_async_copy(zbuf, eblk.at[s, pl.ds(pl.multiple_of(k * G, G), G), :], zsem.at[0])
+
+    w_copy(0, 0).start()
+    zbuf[...] = jnp.zeros_like(zbuf)
     offsets(cnt_ref, ng, eoff, est, boff, nsb_g)
-    nh = (est[NE] + TM // G - 1) // (TM // G)
-
-    def h_start(t, _):
-        h_copy(t).start()
-        return 0
-
-    def h_wait(t, _):
-        h_copy(t).wait()
-        return 0
-
-    lax.fori_loop(0, nh, h_start, 0)
+    nt = jnp.int32(0)
+    for e in range(NE):
+        rows_g = est[e + 1] - est[e]
+        tiles = (rows_g + TM // G - 1) // (TM // G)
+
+        def note(m, _, e=e, nt=nt, rows_g=rows_g):
+            trow[nt + m] = est[e] + m * (TM // G)
+            tnum[nt + m] = jnp.minimum(rows_g - m * (TM // G), TM // G)
+            return 0
+
+        lax.fori_loop(0, tiles, note, 0)
+        nt = nt + tiles
+
+    @pl.when(nt > 0)
+    def _():
+        h_copy(0, 0).start()
+
+    w_copy(1, 1).start()
+    w_copy(2, 2).start()
+
+    def seg_note(q, _):
+        def one(g, _):
+            gdst[eoff[q] + g] = (q // NE) * 256 + boff[q] + g
+            return 0
+
+        return lax.fori_loop(0, ng[q], one, 0)
+
+    lax.fori_loop(0, NSB * NE, seg_note, 0)
+    for s in range(NSB):
+        def zero(k, _, s=s):
+            z_copy(s, k).start()
+            return 0
+
+        lax.fori_loop(nsb_g[s], KC // G, zero, 0)
+
     most = jnp.maximum(jnp.maximum(nsb_g[0], nsb_g[1]), jnp.maximum(nsb_g[2], nsb_g[3]))
     over = most > KC // G
+
+    def g_wait(slot, n):
+        def one(j, _):
+            pltpu.make_async_copy(tbuf.at[slot, pl.ds(0, G), :], eblk.at[0, pl.ds(0, G), :], gsem.at[slot]).wait()
+            return 0
+
+        lax.fori_loop(0, n, one, 0)
+
+    def expert(e, t):
+        ws = lax.rem(e, 3)
+        w_copy(e, ws).wait()
+
+        def tile(m, t):
+            slot = lax.rem(t, 2)
+
+            @pl.when(t + 1 < nt)
+            def _():
+                h_copy(t + 1, 1 - slot).start()
+
+            @pl.when(t >= 2)
+            def _():
+                g_wait(slot, tnum[jnp.maximum(t - 2, 0)])
+
+            h_copy(t, slot).wait()
+            n = tnum[t]
+            for size in (64, 128, 192, 256):
+                @pl.when((n > size // G - 4) & (n <= size // G))
+                def _(size=size):
+                    for c in range(D // 512):
+                        cols = slice(c * 512, c * 512 + 512)
+                        tbuf[slot, :size, cols] = jnp.dot(hs[slot, :size, :], wbuf[ws, :, cols], preferred_element_type=F32).astype(BF16)
+
+            def put(j, _):
+                at = gdst[trow[t] + j]
+                s, k = at // 256, at % 256
+                src = tbuf.at[slot, pl.ds(pl.multiple_of(j * G, G), G), :]
+
+                @pl.when(k < KC // G)
+                def _():
+                    pltpu.make_async_copy(src, eblk.at[s, pl.ds(pl.multiple_of(k * G, G), G), :], gsem.at[slot]).start()
+
+                @pl.when(k >= KC // G)
+                def _():
+                    pltpu.make_async_copy(src, eover.at[s, pl.ds(pl.multiple_of(k * G - KC, G), G), :], gsem.at[slot]).start()
+
+                return 0
+
+            lax.fori_loop(0, n, put, 0)
+            return t + 1
+
+        t = lax.fori_loop(0, (est[e + 1] - est[e] + TM // G - 1) // (TM // G), tile, t)
+
+        @pl.when(e + 3 < NE)
+        def _():
+            w_copy(e + 3, ws).start()
+
+        return t
+
+    lax.fori_loop(0, NE, expert, jnp.int32(0))
+    for back in (1, 2):
+        @pl.when(nt >= back)
+        def _(back=back):
+            t = jnp.maximum(nt - back, 0)
+            g_wait(lax.rem(t, 2), tnum[t])
+
+    for s in range(NSB):
+        def zero_wait(k, _, s=s):
+            z_copy(s, k).wait()
+            return 0
+
+        lax.fori_loop(nsb_g[s], KC // G, zero_wait, 0)
 
     @pl.when(over)
     def _():
@@ -262,107 +359,44 @@
             return lax.fori_loop(0, ng[q], build, 0)
 
         lax.fori_loop(0, NSB * NE, segment, 0)
-
-    kbuf[...] = jnp.zeros_like(kbuf)
-    lax.fori_loop(0, nh, h_wait, 0)
-
-    core = core_ref[0]
-
-    def out_copies(c, s):
-        rel = core_ref[1 + s]
+        core = core_ref[0]
         keep = pl.multiple_of(core * 256, 256)
         give = pl.multiple_of(256 - core * 256, 256)
-        out = []
-        for i in range(CW // RC):
-            cols = pl.ds(i * RC, RC)
-            j = c * (CW // RC) + i
-            out.append(pltpu.make_async_copy(abuf.at[pl.ds(give, 256), cols], theirs.at[j, rel], osem.at[i, 0]))
-            out.append(pltpu.make_async_copy(abuf.at[pl.ds(keep, 256), cols], mine.at[j, rel], osem.at[i, 1]))
-        return out
-
-    def k_copies(c, s, slot):
-        return [pltpu.make_async_copy(kbuf.at[slot, pl.ds(0, KC), pl.ds(i * RC, RC)], eblk.at[c * (CW // RC) + i, s], ksem.at[slot, i]) for i in range(CW // RC)]
-
-    def column(c, _):
-        def expert(e, _):
-            st = c * NE + e
-            ws = st % 3
-            w_copy(st, ws).wait()
-            base = est[e] * G
-            rows = est[e + 1] * G - base
-
-            def work(row, size):
-                row = pl.multiple_of(row, G)
-                ebuf[pl.ds(row, size), :] = jnp.dot(hs[pl.ds(row, size), :], wbuf[ws], preferred_element_type=F32).astype(BF16)
-
-            full = rows // TM
-
-            def body(m, _):
-                work(base + m * TM, TM)
+
+        def piece(q, _):
+            s, c = q // (D // CW), q % (D // CW)
+            rel = core_ref[1 + s]
+            get = pltpu.make_async_copy(eover.at[s, :, pl.ds(pl.multiple_of(c * CW, CW), CW)], kbuf, ksem.at[0])
+            get.start()
+            get.wait()
+
+            def clear(k, _):
+                kbuf[pl.ds(pl.multiple_of(k * G, G), G), :] = jnp.zeros((G, CW), BF16)
                 return 0
 
-            lax.fori_loop(0, full, body, 0)
-            rem = rows - full * TM
-            for size in (64, 128, 192, 256):
-                @pl.when((rem > size - 64) & (rem <= size))
-                def _(size=size):
-                    work(base + full * TM, size)
-
-            @pl.when(st + 3 < steps)
-            def _():
-                w_copy(st + 3, ws).start()
-
+            lax.fori_loop(jnp.maximum(nsb_g[s] - KC // G, 0), KX // G, clear, 0)
+            abuf[...] = jnp.zeros_like(abuf)
+
+            def part(kt, _):
+                rows = pl.ds(pl.multiple_of(kt * TM, TM), TM)
+                for i in range(3):
+                    abuf[...] += lax.dot_general(pbuf[s, i, rows, :], kbuf[rows, :], (((0,), (0,)), ((), ())), preferred_element_type=F32)
+                return 0
+
+            lax.fori_loop(0, KX // TM, part, 0)
+            copies = []
+            for i in range(CW // RC):
+                cols = pl.ds(i * RC, RC)
+                j = c * (CW // RC) + i
+                copies.append(pltpu.make_async_copy(abuf.at[pl.ds(give, 256), cols], theirs.at[j, rel], osem.at[i, 0]))
+                copies.append(pltpu.make_async_copy(abuf.at[pl.ds(keep, 256), cols], mine.at[j, rel], osem.at[i, 1]))
+            for cp in copies:
+                cp.start()
+            for cp in copies:
+                cp.wait()
             return 0
 
-        lax.fori_loop(0, NE, expert, 0)
-
-        def block(s, _):
-            slot = s % 2
-
-            @pl.when(c * NSB + s >= 2)
-            def _():
-                for cp in k_copies(c, s, slot):
-                    cp.wait()
-
-            def segment(e, _):
-                def move(g, _):
-                    row = pl.multiple_of((boff[s * NE + e] + g) * G, G)
-                    src = pl.multiple_of((eoff[s * NE + e] + g) * G, G)
-                    kbuf[slot, pl.ds(row, G), :] = ebuf[pl.ds(src, G), :]
-                    return 0
-
-                return lax.fori_loop(0, ng[s * NE + e], move, 0)
-
-            lax.fori_loop(0, NE, segment, 0)
-            for cp in k_copies(c, s, slot):
-                cp.start()
-
-            @pl.when(over)
-            def _():
-                nk = (nsb_g[s] + TM // G - 1) // (TM // G)
-                abuf[...] = jnp.zeros_like(abuf)
-
-                def tile(kt, _):
-                    ek = kbuf[slot, pl.ds(pl.multiple_of(kt * TM, TM), TM), :]
-                    rows = pl.ds(pl.multiple_of(kt * TM - KC, TM), TM)
-                    for i in range(3):
-                        abuf[...] += lax.dot_general(pbuf[s, i, rows, :], ek, (((0,), (0,)), ((), ())), preferred_element_type=F32)
-                    return 0
-
-                lax.fori_loop(KC // TM, nk, tile, 0)
-                for cp in out_copies(c, s):
-                    cp.start()
-                for cp in out_copies(c, s):
-                    cp.wait()
-
-            return 0
-
-        return lax.fori_loop(0, NSB, block, 0)
-
-    lax.fori_loop(0, D // CW, column, 0)
-    for s in (NSB - 2, NSB - 1):
-        for cp in k_copies(D // CW - 1, s, s % 2):
-            cp.wait()
+        lax.fori_loop(0, NSB * (D // CW), piece, 0)
 
 
 def down_call(cnt, core, rank, wts, h, w2):
@@ -372,15 +406,16 @@
     out = jax.ShapeDtypeStruct((NC, NSB, 256, RC), F32)
     return pl.pallas_call(
         down_kernel,
-        out_shape=(jax.ShapeDtypeStruct((NC, NSB, KC, RC), BF16), out, out),
+        out_shape=(jax.ShapeDtypeStruct((NSB, KC, D), BF16), jax.ShapeDtypeStruct((NSB, KX, D), BF16), out, out),
         in_specs=[smem, smem, vmem, vmem, any_spec, any_spec],
-        out_specs=(any_spec, any_spec, any_spec),
+        out_specs=(any_spec, any_spec, any_spec, any_spec),
         scratch_shapes=[
-            pltpu.VMEM((XR, FF), BF16),
-            pltpu.VMEM((XR, CW), BF16),
-            pltpu.VMEM((2, SBR, CW), BF16),
+            pltpu.VMEM((2, TM, FF), BF16),
+            pltpu.VMEM((3, FF, D), BF16),
+            pltpu.VMEM((2, TM, D), BF16),
+            pltpu.VMEM((G, D), BF16),
+            pltpu.VMEM((KX, CW), BF16),
             pltpu.VMEM((NSB, 3, KX, SB), BF16),
-            pltpu.VMEM((3, FF, CW), BF16),
             pltpu.VMEM((SB, CW), F32),
             pltpu.VMEM((3, NSB, NE, SB), F32),
             pltpu.SMEM((NSB * NE,), jnp.int32),
@@ -388,10 +423,15 @@
             pltpu.SMEM((NE + 1,), jnp.int32),
             pltpu.SMEM((NSB * NE,), jnp.int32),
             pltpu.SMEM((NSB,), jnp.int32),
+            pltpu.SMEM((XG,), jnp.int32),
+            pltpu.SMEM((64,), jnp.int32),
+            pltpu.SMEM((64,), jnp.int32),
+            pltpu.SemaphoreType.DMA((2,)),
+            pltpu.SemaphoreType.DMA((3,)),
+            pltpu.SemaphoreType.DMA((2,)),
             pltpu.SemaphoreType.DMA((1,)),
-            pltpu.SemaphoreType.DMA((3,)),
             pltpu.SemaphoreType.DMA((CW // RC, 2)),
-            pltpu.SemaphoreType.DMA((2, CW // RC)),
+            pltpu.SemaphoreType.DMA((1,)),
         ],
         compiler_params=pltpu.CompilerParams(vmem_limit_bytes=VMEM_LIMIT),
         cost_estimate=pl.CostEstimate(flops=40_000_000_000, bytes_accessed=100_000_000, transcendentals=0),
@@ -599,7 +639,7 @@
         return (pltpu.make_async_copy(theirs.at[j], give.at[j], load.at[0, j]), pltpu.make_async_copy(mine.at[j], own.at[j], load.at[1, j]))
 
     def e_of(j, slot):
-        return pltpu.make_async_copy(eblk.at[j], ev.at[slot], esem.at[slot])
+        return pltpu.make_async_copy(eblk.at[:, :, pl.ds(pl.multiple_of(j * RC, RC), RC)], ev.at[slot], esem.at[slot])
 
     def core_of(j):
         return remote(give.at[j], r1.at[j], send.at[0, j], recv.at[0, j], pn)
@@ -760,7 +800,7 @@
         place = jnp.where(other_x, jnp.where(other_y, 2, 1), jnp.where(other_y, 3, 0))
         core = jnp.concatenate([(me % 2)[None], place]).astype(jnp.int32)
         h = up_call(cnt, rank, ball, w1_experts, w3_experts)
-        eblk, mine, theirs = down_call(cnt, core, rank, wsb, h, w2_experts)
+        eblk, _, mine, theirs = down_call(cnt, core, rank, wsb, h, w2_experts)
         return return_call(cnt, pt, eblk, mine, theirs, hidden, shared_out)
 
     return jax.shard_map(local_fn, mesh=mesh, in_specs=(tok_spec, P(), P(), P(), P(), P(), expert_spec, expert_spec, expert_spec, tok_spec), out_specs=tok_spec, check_vma=False)

time: 277 us -> 260 us (0.939)
  Pallas kernels: 265 us -> 248 us
    pallas_call x1, Pallas kernels: 66 us -> 56.1 us  [up_call(): pl.pallas_call(up_kernel, out_shape=jax.ShapeDtypeStruct((XR, FF), BF16),...]
    pallas_call x1, Pallas kernels: 43.5 us -> 36.8 us  [down_call(): pl.pallas_call(down_kernel, out_shape=(jax.ShapeDtypeStruct((NSB, KC, D),...]
where the time goes in v2:
time: 260 us; the launch traced here: 259 us
  Pallas kernels  248 us (95%)
  other arithmetic  6.15 us (2%)
  local copies, waits for them, and re-layouts  4.96 us (2%)
    pallas_call x1, Pallas kernels, return_call(): pl.pallas_call(return_kernel, out_shape=jax.ShapeDtypeStruct((T, D), BF16...  101 us
    pallas_call x1, Pallas kernels, up_call(): pl.pallas_call(up_kernel, out_shape=jax.ShapeDtypeStruct((XR, FF), BF16),...  56.1 us
    pallas_call x1, Pallas kernels, gather_call(): pl.pallas_call(gather_kernel, out_shape=(jax.ShapeDtypeStruct((8 * T, D),...  54.3 us
    pallas_call x1, Pallas kernels, down_call(): pl.pallas_call(down_kernel, out_shape=(jax.ShapeDtypeStruct((NSB, KC, D),...  36.8 us

profile of v2, /device:TPU:0, one launch (start us, length us, event | category | flops | bytes accessed | tf_op | source)
XLA Modules:
  0.0 259.4 jit_solution(7952162876387486129)
XLA Ops:
  0.0 0.0 copy-start
  0.0 0.7 pad_add_fusion.core_ref
  0.7 1.7 fusion
  2.3 0.7 convert_element_type.10
  3.0 0.7 fusion.3
  3.8 1.7 fusion.2.b_any.b_ref
  5.5 0.0 copy-start.2
  5.5 1.0 copy-done.2
  6.5 0.0 copy-done
  6.5 0.5 fusion.5
  7.1 0.6 select_bitcast_fusion.wts_ref
  7.8 54.3 %gather.1 = (bf16[2048,2560]{1,0:T(8,128)(2,1)}, f32[4,8,512]{2,1,0:T(8,128)}, s32[4,8,512]{2,1,0:T(8,128)}, s32[4,8,128]{2,1,0:T(8,128)}, bf16[4,3,512,768]{3,2,1,0:T(8,128)(2,1)}, /*index=5*/bf16[256,2560]{1,0:T(8,128)(2,1)}) custom-call(bf16[256,2560]{1,0:T(8,128)(2,1)} %copy-done.2, bf16[256,2560]{1,0:T(8,128)(2,1)} %copy-done.2, ...), custom_call_target="tpu_custom_call" | custom-call | flops 12000000000 | bytes 60000000 | tf_op jit(solution)/shard_map/gather/pallas_call | solution.py:600
  62.0 1.4 slice_reduce_fusion.cnt_ref
  63.5 56.1 %up.1.h = bf16[6912,1536]{1,0:T(8,128)(2,1)} custom-call(s32[4,8]{1,0:T(4,128)} %slice_reduce_fusion.cnt_ref, s32[4,8,512]{2,1,0:T(8,128)} %get-tuple-element.16.rank_ref, bf16[2048,2560]{1,0:T(8,128)(2,1)} %get-tuple-element.18.ball, bf16[8,2560,1536]{2,1,0:T(8,128)(2,1)} %w1.3, bf16[8,2560,1536]{2,1,0:T(8,128)(2,1)} %w3.3), custom_call_target="tpu_custom_call" | custom-call | flops 48000000000 | bytes 140000000 | tf_op jit(solution)/shard_map/up/pallas_call | solution.py:178
  119.6 36.8 %down.1 = (bf16[4,768,2560]{2,1,0:T(8,128)(2,1)}, bf16[4,1024,2560]{2,1,0:T(8,128)(2,1)}, f32[10,4,256,256]{3,2,1,0:T(8,128)}, f32[10,4,256,256]{3,2,1,0:T(8,128)}) custom-call(s32[4,8]{1,0:T(4,128)} %slice_reduce_fusion.cnt_ref, s32[5]{0:T(128)} %pad_add_fusion.core_ref, s32[4,8,512]{2,1,0:T(8,128)} %get-tuple-element.16.rank_ref, ...), custom_call_target="tpu_custom_call" | custom-call | flops 40000000000 | bytes 100000000 | tf_op jit(solution)/shard_map/down/pallas_call | solution.py:407
  156.4 0.0 copy-start.1
  156.4 100.5 %return_sum.1 = bf16[256,2560]{1,0:T(8,128)(2,1)} custom-call(s32[4,8]{1,0:T(4,128)} %slice_reduce_fusion.cnt_ref, bf16[4,3,512,768]{3,2,1,0:T(8,128)(2,1)} %get-tuple-element.15.pt, bf16[4,768,2560]{2,1,0:T(8,128)(2,1)} %get-tuple-element.19.eblk, f32[10,4,256,256]{3,2,1,0:T(8,128)} %get-tuple-element.20.mine, ...), custom_call_target="tpu_custom_call" | custom-call | tf_op jit(solution)/shard_map/return_sum/pallas_call | solution.py:760
  256.9 2.5 copy.14
  259.4 0.0 copy-done.1
  (3 shorter events, 0.1 us)
Async XLA Ops:
  0.0 6.5 %copy-start = (bf16[2560,64]{0,1:T(8,128)(2,1)S(1)}, bf16[2560,64]{0,1:T(8,128)(2,1)}, u32[]{:S(2)}) copy-start(bf16[2560,64]{0,1:T(8,128)(2,1)} %param.12) | copy-start | bytes 983044
  5.5 1.1 copy-start.2
  156.4 103.0 %copy-start.1 = (bf16[2560,64]{0,1:T(8,128)(2,1)S(1)}, bf16[2560,64]{0,1:T(8,128)(2,1)}, u32[]{:S(2)}) copy-start(bf16[2560,64]{0,1:T(8,128)(2,1)} %param.12) | copy-start | bytes 983044

commit v3 on v2

--- a/solution.py
+++ b/solution.py
@@ -17,7 +17,9 @@
 SB = 512
 G = 16
 TM = 256
-XG = 432
+LM = 384
+SIZES = tuple(range(64, LM + 1, 64))
+XG = 440
 XR = XG * G
 SBR = 1792
 FC = 512
@@ -31,6 +33,7 @@
 NC = D // RC
 KC = 768
 KX = SBR - KC
+LAG = 2
 VMEM_LIMIT = 66000000
 BF16 = jnp.bfloat16
 F32 = jnp.float32
@@ -116,7 +119,7 @@
         return pltpu.make_async_copy(hbuf.at[hs, pl.ds(0, size), :], h_out.at[pl.ds(row, size), pl.ds(col, FC)], hsem.at[0])
 
     def wait_h(quarters):
-        for q in range(1, 5):
+        for q in range(1, LM // 64 + 1):
             @pl.when(quarters == q)
             def _(q=q):
                 h_copy(0, 0, 0, q * 64).wait()
@@ -147,7 +150,7 @@
             last[0] = size // 64
             h_copy(hs, row, col, size).start()
 
-        full = rows // TM
+        full = jnp.maximum(rows - LM + TM - 1, 0) // TM
 
         def body(m, k):
             work(base + m * TM, TM, k)
@@ -156,7 +159,7 @@
         k = lax.fori_loop(0, full, body, k)
         rem = rows - full * TM
         at = base + full * TM
-        for size in (64, 128, 192, 256):
+        for size in SIZES:
             @pl.when((rem > size - 64) & (rem <= size))
             def _(size=size):
                 work(at, size, k)
@@ -186,7 +189,7 @@
             pltpu.VMEM((SBR, SB), BF16),
             pltpu.VMEM((TM, DH), BF16),
             pltpu.VMEM((3, 2, D, FC), BF16),
-            pltpu.VMEM((2, TM, FC), BF16),
+            pltpu.VMEM((2, LM, FC), BF16),
             pltpu.SMEM((NSB * NE,), jnp.int32),
             pltpu.SMEM((NSB * NE,), jnp.int32),
             pltpu.SMEM((NE + 1,), jnp.int32),
@@ -210,10 +213,13 @@
         return pltpu.make_async_copy(w2.at[e], wbuf.at[slot], wsem.at[slot])
 
     def h_copy(t, slot):
-        return pltpu.make_async_copy(h.at[pl.ds(pl.multiple_of(trow[t] * G, G), TM), :], hs.at[slot], hsem.at[slot])
+        return pltpu.make_async_copy(h.at[pl.ds(pl.multiple_of(trow[t] * G, G), LM), :], hs.at[slot], hsem.at[slot])
 
     def z_copy(s, k):
         return pltpu.make_async_copy(zbuf, eblk.at[s, pl.ds(pl.multiple_of(k * G, G), G), :], zsem.at[0])
+
+    def tiles_of(rows_g):
+        return jnp.maximum(rows_g - LM // G + TM // G - 1, 0) // (TM // G) + jnp.where(rows_g > 0, 1, 0)
 
     w_copy(0, 0).start()
     zbuf[...] = jnp.zeros_like(zbuf)
@@ -221,11 +227,11 @@
     nt = jnp.int32(0)
     for e in range(NE):
         rows_g = est[e + 1] - est[e]
-        tiles = (rows_g + TM // G - 1) // (TM // G)
-
-        def note(m, _, e=e, nt=nt, rows_g=rows_g):
+        tiles = tiles_of(rows_g)
+
+        def note(m, _, e=e, nt=nt, rows_g=rows_g, tiles=tiles):
             trow[nt + m] = est[e] + m * (TM // G)
-            tnum[nt + m] = jnp.minimum(rows_g - m * (TM // G), TM // G)
+            tnum[nt + m] = jnp.where(m == tiles - 1, rows_g - m * (TM // G), TM // G)
             return 0
 
         lax.fori_loop(0, tiles, note, 0)
@@ -280,7 +286,7 @@
 
             h_copy(t, slot).wait()
             n = tnum[t]
-            for size in (64, 128, 192, 256):
+            for size in SIZES:
                 @pl.when((n > size // G - 4) & (n <= size // G))
                 def _(size=size):
                     for c in range(D // 512):
@@ -305,7 +311,7 @@
             lax.fori_loop(0, n, put, 0)
             return t + 1
 
-        t = lax.fori_loop(0, (est[e + 1] - est[e] + TM // G - 1) // (TM // G), tile, t)
+        t = lax.fori_loop(0, tiles_of(est[e + 1] - est[e]), tile, t)
 
         @pl.when(e + 3 < NE)
         def _():
@@ -410,9 +416,9 @@
         in_specs=[smem, smem, vmem, vmem, any_spec, any_spec],
         out_specs=(any_spec, any_spec, any_spec, any_spec),
         scratch_shapes=[
-            pltpu.VMEM((2, TM, FF), BF16),
+            pltpu.VMEM((2, LM, FF), BF16),
             pltpu.VMEM((3, FF, D), BF16),
-            pltpu.VMEM((2, TM, D), BF16),
+            pltpu.VMEM((2, LM, D), BF16),
             pltpu.VMEM((G, D), BF16),
             pltpu.VMEM((KX, CW), BF16),
             pltpu.VMEM((NSB, 3, KX, SB), BF16),
@@ -732,8 +738,9 @@
     for c in pt_copies:
         c.start()
     e_of(1, 1).start()
+    begin(0)
+    begin(1)
     enter([pn, xn, yn])
-    each(begin)
     for c in pt_copies:
         c.wait()
 
@@ -743,12 +750,23 @@
         @pl.when(j + 2 < NC)
         def _():
             e_of(j + 2, lax.rem(j, 2)).start()
+            begin(j + 2)
 
         pair(j)
+
+        @pl.when(j >= LAG)
+        def _():
+            onward(j - LAG)
+
         return 0
 
     lax.fori_loop(0, NC, steady, 0)
-    each(onward)
+
+    def last(j, _):
+        onward(j)
+        return 0
+
+    lax.fori_loop(NC - LAG, NC, last, 0)
     each(finish)
     each(drain)
 

time: 260 us -> 262 us (level)
  Pallas kernels: 248 us -> 251 us
    pallas_call x1, Pallas kernels: 101 us -> 104 us  [return_call(): pl.pallas_call(return_kernel, out_shape=jax.ShapeDtypeStruct((T, D), BF16...]
where the time goes in v3:
time: 262 us; the launch traced here: 263 us
  Pallas kernels  251 us (96%)
  other arithmetic  6.14 us (2%)
  local copies, waits for them, and re-layouts  4.96 us (2%)
    pallas_call x1, Pallas kernels, return_call(): pl.pallas_call(return_kernel, out_shape=jax.ShapeDtypeStruct((T, D), BF16...  104 us
    pallas_call x1, Pallas kernels, up_call(): pl.pallas_call(up_kernel, out_shape=jax.ShapeDtypeStruct((XR, FF), BF16),...  55.7 us
    pallas_call x1, Pallas kernels, gather_call(): pl.pallas_call(gather_kernel, out_shape=(jax.ShapeDtypeStruct((8 * T, D),...  54.3 us
    pallas_call x1, Pallas kernels, down_call(): pl.pallas_call(down_kernel, out_shape=(jax.ShapeDtypeStruct((NSB, KC, D),...  36.9 us

profile of v3, /device:TPU:0, one launch (start us, length us, event | category | flops | bytes accessed | tf_op | source)
XLA Modules:
  0.0 262.6 jit_solution(3289624248602213038)
XLA Ops:
  0.0 0.0 copy-start
  0.0 0.7 pad_add_fusion.core_ref
  0.7 1.7 fusion
  2.3 0.7 convert_element_type.10
  3.0 0.7 fusion.3
  3.8 1.7 fusion.2.b_any.b_ref
  5.5 0.0 copy-start.2
  5.5 1.0 copy-done.2
  6.5 0.0 copy-done
  6.5 0.5 fusion.5
  7.1 0.6 select_bitcast_fusion.wts_ref
  7.8 54.3 %gather.1 = (bf16[2048,2560]{1,0:T(8,128)(2,1)}, f32[4,8,512]{2,1,0:T(8,128)}, s32[4,8,512]{2,1,0:T(8,128)}, s32[4,8,128]{2,1,0:T(8,128)}, bf16[4,3,512,768]{3,2,1,0:T(8,128)(2,1)}, /*index=5*/bf16[256,2560]{1,0:T(8,128)(2,1)}) custom-call(bf16[256,2560]{1,0:T(8,128)(2,1)} %copy-done.2, bf16[256,2560]{1,0:T(8,128)(2,1)} %copy-done.2, ...), custom_call_target="tpu_custom_call" | custom-call | flops 12000000000 | bytes 60000000 | tf_op jit(solution)/shard_map/gather/pallas_call | solution.py:606
  62.0 1.4 slice_reduce_fusion.cnt_ref
  63.5 55.7 %up.1.h = bf16[7040,1536]{1,0:T(8,128)(2,1)} custom-call(s32[4,8]{1,0:T(4,128)} %slice_reduce_fusion.cnt_ref, s32[4,8,512]{2,1,0:T(8,128)} %get-tuple-element.16.rank_ref, bf16[2048,2560]{1,0:T(8,128)(2,1)} %get-tuple-element.18.ball, bf16[8,2560,1536]{2,1,0:T(8,128)(2,1)} %w1.3, bf16[8,2560,1536]{2,1,0:T(8,128)(2,1)} %w3.3), custom_call_target="tpu_custom_call" | custom-call | flops 48000000000 | bytes 140000000 | tf_op jit(solution)/shard_map/up/pallas_call | solution.py:181
  119.2 36.9 %down.1 = (bf16[4,768,2560]{2,1,0:T(8,128)(2,1)}, bf16[4,1024,2560]{2,1,0:T(8,128)(2,1)}, f32[10,4,256,256]{3,2,1,0:T(8,128)}, f32[10,4,256,256]{3,2,1,0:T(8,128)}) custom-call(s32[4,8]{1,0:T(4,128)} %slice_reduce_fusion.cnt_ref, s32[5]{0:T(128)} %pad_add_fusion.core_ref, s32[4,8,512]{2,1,0:T(8,128)} %get-tuple-element.16.rank_ref, ...), custom_call_target="tpu_custom_call" | custom-call | flops 40000000000 | bytes 100000000 | tf_op jit(solution)/shard_map/down/pallas_call | solution.py:413
  156.0 0.0 copy-start.1
  156.0 104.1 %return_sum.1 = bf16[256,2560]{1,0:T(8,128)(2,1)} custom-call(s32[4,8]{1,0:T(4,128)} %slice_reduce_fusion.cnt_ref, bf16[4,3,512,768]{3,2,1,0:T(8,128)(2,1)} %get-tuple-element.15.pt, bf16[4,768,2560]{2,1,0:T(8,128)(2,1)} %get-tuple-element.19.eblk, f32[10,4,256,256]{3,2,1,0:T(8,128)} %get-tuple-element.20.mine, ...), custom_call_target="tpu_custom_call" | custom-call | tf_op jit(solution)/shard_map/return_sum/pallas_call | solution.py:778
  260.1 2.5 copy.14
  262.6 0.0 copy-done.1
  (3 shorter events, 0.1 us)
Async XLA Ops:
  0.0 6.5 %copy-start = (bf16[2560,64]{0,1:T(8,128)(2,1)S(1)}, bf16[2560,64]{0,1:T(8,128)(2,1)}, u32[]{:S(2)}) copy-start(bf16[2560,64]{0,1:T(8,128)(2,1)} %param.12) | copy-start | bytes 983044
  5.5 1.1 copy-start.2
  156.0 106.6 %copy-start.1 = (bf16[2560,64]{0,1:T(8,128)(2,1)S(1)}, bf16[2560,64]{0,1:T(8,128)(2,1)}, u32[]{:S(2)}) copy-start(bf16[2560,64]{0,1:T(8,128)(2,1)} %param.12) | copy-start | bytes 983044

commit v4 on v0

--- a/solution.py
+++ b/solution.py
@@ -17,17 +17,26 @@
 SB = 512
 G = 16
 TM = 256
-XG = 432
+LM = 384
+SIZES = tuple(range(64, LM + 1, 64))
+XG = 440
 XR = XG * G
 SBR = 1792
 FC = 512
 NF = FF // FC
+DH = D // 2
 T = 256
 SHARED = 3072
 SF = 256
 CW = 512
 RC = 256
 NC = D // RC
+KC = 768
+HR = 1280
+NK = KC // G
+NOROW = NE * LM // G
+WS = 4
+LAG = 2
 VMEM_LIMIT = 66000000
 BF16 = jnp.bfloat16
 F32 = jnp.float32
@@ -57,7 +66,7 @@
         nsb_g[s] = b
 
 
-def up_kernel(cnt_ref, rank_ref, ball, w1, w3, h_out, xs, bbuf, pbuf, tbuf, wbuf, hbuf, ng, eoff, est, boff, nsb_g, dst, last, bsem, wsem, hsem):
+def up_kernel(cnt_ref, rank_ref, ball, w1, w3, h_out, table, xs, bbuf, pbuf, tbuf, wbuf, hbuf, ng, eoff, est, boff, nsb_g, dst, last, bsem, wsem, hsem):
     def w_copies(step, slot):
         e = step // NF
         f = step % NF
@@ -65,21 +74,18 @@
         return (pltpu.make_async_copy(w1.at[e, :, cols], wbuf.at[slot, 0], wsem.at[slot, 0]),
                 pltpu.make_async_copy(w3.at[e, :, cols], wbuf.at[slot, 1], wsem.at[slot, 1]))
 
-    def b_copy(s, slot):
-        return pltpu.make_async_copy(ball.at[pl.ds(s * SB, SB), :], bbuf.at[slot], bsem.at[slot])
+    def b_copy(s, half):
+        return pltpu.make_async_copy(ball.at[pl.ds(s * SB, SB), pl.ds(half * DH, DH)], bbuf.at[half], bsem.at[half])
 
     b_copy(0, 0).start()
-    for c in w_copies(0, 0):
-        c.start()
-    for c in w_copies(1, 1):
-        c.start()
+    b_copy(0, 1).start()
+    for st in range(3):
+        for c in w_copies(st, st):
+            c.start()
     offsets(cnt_ref, ng, eoff, est, boff, nsb_g)
     rows16 = lax.broadcasted_iota(jnp.int32, (G, SB), 0)
 
     for s in range(NSB):
-        slot = s % 2
-        if s + 1 < NSB:
-            b_copy(s + 1, 1 - slot).start()
         for e in range(NE):
             rk = jnp.broadcast_to(rank_ref[s, e:e + 1, :], (G, SB))
 
@@ -91,35 +97,67 @@
                 return 0
 
             lax.fori_loop(0, ng[s * NE + e], build, 0)
-        b_copy(s, slot).wait()
-
-        def tile(m, _, s=s, slot=slot):
-            prow = pbuf[pl.ds(pl.multiple_of(m * TM, TM), TM), :]
-            for n in range(D // 512):
-                cols = slice(n * 512, (n + 1) * 512)
-                tbuf[:, cols] = jnp.dot(prow, bbuf[slot, :, cols], preferred_element_type=F32).astype(BF16)
-
-            def put(j, _):
-                row = pl.multiple_of(dst[m * (TM // G) + j] * G, G)
-                xs[pl.ds(row, G), :] = tbuf[pl.ds(pl.multiple_of(j * G, G), G), :]
+        for half in range(2):
+            b_copy(s, half).wait()
+
+            def tile(m, _, s=s, half=half):
+                prow = pbuf[pl.ds(pl.multiple_of(m * TM, TM), TM), :]
+                for n in range(5):
+                    cols = slice(n * 256, (n + 1) * 256)
+                    tbuf[:, cols] = jnp.dot(prow, bbuf[half, :, cols], preferred_element_type=F32).astype(BF16)
+
+                def put(j, _):
+                    row = pl.multiple_of(dst[m * (TM // G) + j] * G, G)
+                    xs[pl.ds(row, G), half * DH:(half + 1) * DH] = tbuf[pl.ds(pl.multiple_of(j * G, G), G), :]
+                    return 0
+
+                lax.fori_loop(0, jnp.minimum(TM // G, nsb_g[s] - m * (TM // G)), put, 0)
                 return 0
 
-            lax.fori_loop(0, jnp.minimum(TM // G, nsb_g[s] - m * (TM // G)), put, 0)
-            return 0
-
-        lax.fori_loop(0, (nsb_g[s] + TM // G - 1) // (TM // G), tile, 0)
-
-    def h_copy(hs, row, col, size):
-        return pltpu.make_async_copy(hbuf.at[hs, pl.ds(0, size), :], h_out.at[pl.ds(row, size), pl.ds(col, FC)], hsem.at[0])
+            lax.fori_loop(0, (nsb_g[s] + TM // G - 1) // (TM // G), tile, 0)
+            if s + 1 < NSB:
+                b_copy(s + 1, half).start()
+
+    def fill(k, _):
+        table[k] = NOROW
+        return 0
+
+    lax.fori_loop(0, NSB * NK, fill, 0)
+    over = jnp.int32(0)
+    for e in range(NE):
+        over = jnp.maximum(over, est[e + 1] - est[e] - LM // G)
+    for s in range(NSB):
+        over = jnp.maximum(over, nsb_g[s] - NK)
+    table[NSB * NK] = over
+
+    def segment(q, _):
+        s, e = q // NE, q % NE
+        first = eoff[q] - est[e]
+
+        def one(g, _):
+            k = boff[q] + g
+
+            @pl.when((k < NK) & (first + g < LM // G))
+            def _():
+                table[s * NK + k] = e * (LM // G) + first + g
+
+            return 0
+
+        return lax.fori_loop(0, ng[q], one, 0)
+
+    lax.fori_loop(0, NSB * NE, segment, 0)
+
+    def h_copy(hs, e, row, col, size):
+        return pltpu.make_async_copy(hbuf.at[hs, pl.ds(0, size), :], h_out.at[e, pl.ds(row, size), pl.ds(col, FC)], hsem.at[0])
 
     def wait_h(quarters):
-        for q in range(1, 5):
+        for q in range(1, LM // 64 + 1):
             @pl.when(quarters == q)
             def _(q=q):
-                h_copy(0, 0, 0, q * 64).wait()
+                h_copy(0, 0, 0, 0, q * 64).wait()
 
     def step(st, k):
-        slot = st % 2
+        slot = lax.rem(st, 3)
         e = st // NF
         col = pl.multiple_of((st % NF) * FC, FC)
         for c in w_copies(st, slot):
@@ -130,19 +168,21 @@
         def work(row, size, k):
             row = pl.multiple_of(row, G)
             hs = k % 2
-            x = xs[pl.ds(row, size), :]
-            gate = jnp.dot(x, wbuf[slot, 0], preferred_element_type=F32)
-            lin = jnp.dot(x, wbuf[slot, 1], preferred_element_type=F32)
-            hbuf[hs, pl.ds(0, size), :] = (jax.nn.silu(gate) * lin).astype(BF16)
+            for n in range(FC // 256):
+                cols = slice(n * 256, (n + 1) * 256)
+                x = xs[pl.ds(row, size), :]
+                gate = jnp.dot(x, wbuf[slot, 0, :, cols], preferred_element_type=F32)
+                lin = jnp.dot(x, wbuf[slot, 1, :, cols], preferred_element_type=F32)
+                hbuf[hs, pl.ds(0, size), cols] = (jax.nn.silu(gate) * lin).astype(BF16)
 
             @pl.when(k > 0)
             def _():
                 wait_h(last[0])
 
             last[0] = size // 64
-            h_copy(hs, row, col, size).start()
-
-        full = rows // TM
+            h_copy(hs, e, pl.multiple_of(row - base, G), col, size).start()
+
+        full = jnp.maximum(rows - LM + TM - 1, 0) // TM
 
         def body(m, k):
             work(base + m * TM, TM, k)
@@ -151,14 +191,14 @@
         k = lax.fori_loop(0, full, body, k)
         rem = rows - full * TM
         at = base + full * TM
-        for size in (64, 128, 192, 256):
+        for size in SIZES:
             @pl.when((rem > size - 64) & (rem <= size))
             def _(size=size):
                 work(at, size, k)
 
-        @pl.when(st + 2 < NE * NF)
+        @pl.when(st + 3 < NE * NF)
         def _():
-            for c in w_copies(st + 2, slot):
+            for c in w_copies(st + 3, slot):
                 c.start()
 
         return k + jnp.where(rem > 0, 1, 0)
@@ -172,16 +212,16 @@
     any_spec = pl.BlockSpec(memory_space=pl.ANY)
     return pl.pallas_call(
         up_kernel,
-        out_shape=jax.ShapeDtypeStruct((XR, FF), BF16),
+        out_shape=(jax.ShapeDtypeStruct((NE, HR, FF), BF16), jax.ShapeDtypeStruct((256,), jnp.int32)),
         in_specs=[pl.BlockSpec(memory_space=pltpu.SMEM), pl.BlockSpec(memory_space=pltpu.VMEM), any_spec, any_spec, any_spec],
-        out_specs=any_spec,
+        out_specs=(any_spec, pl.BlockSpec(memory_space=pltpu.SMEM)),
         scratch_shapes=[
             pltpu.VMEM((XR, D), BF16),
-            pltpu.VMEM((2, SB, D), BF16),
+            pltpu.VMEM((2, SB, DH), BF16),
             pltpu.VMEM((SBR, SB), BF16),
-            pltpu.VMEM((TM, D), BF16),
-            pltpu.VMEM((2, 2, D, FC), BF16),
-            pltpu.VMEM((2, TM, FC), BF16),
+            pltpu.VMEM((TM, DH), BF16),
+            pltpu.VMEM((3, 2, D, FC), BF16),
+            pltpu.VMEM((2, LM, FC), BF16),
             pltpu.SMEM((NSB * NE,), jnp.int32),
             pltpu.SMEM((NSB * NE,), jnp.int32),
             pltpu.SMEM((NE + 1,), jnp.int32),
@@ -190,7 +230,7 @@
             pltpu.SMEM((SBR // G,), jnp.int32),
             pltpu.SMEM((1,), jnp.int32),
             pltpu.SemaphoreType.DMA((2,)),
-            pltpu.SemaphoreType.DMA((2, 2)),
+            pltpu.SemaphoreType.DMA((3, 2)),
             pltpu.SemaphoreType.DMA((1,)),
         ],
         compiler_params=pltpu.CompilerParams(vmem_limit_bytes=VMEM_LIMIT),
@@ -199,7 +239,13 @@
     )(cnt, rank, ball, w1, w3)
 
 
-def down_kernel(cnt_ref, core_ref, rank_ref, wt_ref, h, w2, mine, theirs,
+def down_kernel(table, cnt_ref, core_ref, rank_ref, wt_ref, h, w2, mine, theirs, *scratch):
+    @pl.when(table[NSB * NK] > 0)
+    def _():
+        down_all(cnt_ref, core_ref, rank_ref, wt_ref, h, w2, mine, theirs, *scratch)
+
+
+def down_all(cnt_ref, core_ref, rank_ref, wt_ref, h, w2, mine, theirs,
                 hs, ebuf, kbuf, pbuf, wbuf, abuf, wsplit, ng, eoff, est, boff, nsb_g, hsem, wsem, osem):
     steps = (D // CW) * NE
 
@@ -207,24 +253,18 @@
         col = pl.multiple_of((st // NE) * CW, CW)
         return pltpu.make_async_copy(w2.at[st % NE, :, pl.ds(col, CW)], wbuf.at[slot], wsem.at[slot])
 
-    def h_copy(t):
-        rows = pl.ds(pl.multiple_of(t * TM, TM), TM)
-        return pltpu.make_async_copy(h.at[rows, :], hs.at[rows, :], hsem.at[0])
-
     for st in range(3):
         w_copy(st, st).start()
     offsets(cnt_ref, ng, eoff, est, boff, nsb_g)
-    nh = (est[NE] + TM // G - 1) // (TM // G)
-
-    def h_start(t, _):
-        h_copy(t).start()
-        return 0
-
-    def h_wait(t, _):
-        h_copy(t).wait()
-        return 0
-
-    lax.fori_loop(0, nh, h_start, 0)
+    for e in range(NE):
+        def fetch(m, _, e=e):
+            to = pl.ds(pl.multiple_of(est[e] * G + m * TM, G), TM)
+            copy = pltpu.make_async_copy(h.at[e, pl.ds(pl.multiple_of(m * TM, TM), TM), :], hs.at[to, :], hsem.at[0])
+            copy.start()
+            copy.wait()
+            return 0
+
+        lax.fori_loop(0, (est[e + 1] - est[e] + TM // G - 1) // (TM // G), fetch, 0)
     for s in range(NSB):
         w = wt_ref[s]
         hi = w.astype(BF16).astype(F32)
@@ -255,7 +295,6 @@
 
         lax.fori_loop(nsb_g[s], -(-nsb_g[s] // (TM // G)) * (TM // G), clear, 0)
     kbuf[...] = jnp.zeros_like(kbuf)
-    lax.fori_loop(0, nh, h_wait, 0)
 
     core = core_ref[0]
 
@@ -291,8 +330,8 @@
 
             lax.fori_loop(0, full, body, 0)
             rem = rows - full * TM
-            for size in (64, 128, 192, 256):
-                @pl.when((rem > size - 64) & (rem <= size))
+            for size in (128, 256):
+                @pl.when((rem > size - 128) & (rem <= size))
                 def _(size=size):
                     work(base + full * TM, size)
 
@@ -350,7 +389,7 @@
             cp.wait()
 
 
-def down_call(cnt, core, rank, wts, h, w2):
+def down_call(table, cnt, core, rank, wts, h, w2):
     any_spec = pl.BlockSpec(memory_space=pl.ANY)
     smem = pl.BlockSpec(memory_space=pltpu.SMEM)
     vmem = pl.BlockSpec(memory_space=pltpu.VMEM)
@@ -358,7 +397,7 @@
     return pl.pallas_call(
         down_kernel,
         out_shape=(out, out),
-        in_specs=[smem, smem, vmem, vmem, any_spec, any_spec],
+        in_specs=[smem, smem, smem, vmem, vmem, any_spec, any_spec],
         out_specs=(any_spec, any_spec),
         scratch_shapes=[
             pltpu.VMEM((XR, FF), BF16),
@@ -380,7 +419,7 @@
         compiler_params=pltpu.CompilerParams(vmem_limit_bytes=VMEM_LIMIT),
         cost_estimate=pl.CostEstimate(flops=40_000_000_000, bytes_accessed=100_000_000, transcendentals=0),
         name="down",
-    )(cnt, core, rank, wts, h, w2)
+    )(table, cnt, core, rank, wts, h, w2)
 
 
 def neighbours():
@@ -402,7 +441,7 @@
     pl.semaphore_wait(barrier, len(others))
 
 
-def gather_kernel(b_any, b_ref, wts_ref, w1, w3, w2, ball, wall, s_ref, w13buf, w2buf, acc, send, recv, wsend, wrecv, local, wsem):
+def gather_kernel(b_any, b_ref, wts_ref, w1, w3, w2, ball, wall_out, rank_ref, cnt_ref, pt, s_ref, wall, ptbuf, cols_buf, w13buf, w2buf, acc, send, recv, wsend, wrecv, local, wsem, psem):
     me, pn, xn, yn = neighbours()
     diag = xn + yn - me
     half = T // 2
@@ -475,6 +514,53 @@
     third = [relay(10, xn, 1, pn), relay(11, yn, 0, pn)]
     for c in third:
         c.start()
+    for c in small:
+        c.wait_recv()
+    keep[1].wait()
+    before = jnp.where(lax.broadcasted_iota(jnp.int32, (SB, SB), 0) < lax.broadcasted_iota(jnp.int32, (SB, SB), 1), 1.0, 0.0).astype(BF16)
+    row = lax.broadcasted_iota(jnp.int32, (1, KC), 1)
+    puts = []
+    for s in range(NSB):
+        slot = s % 2
+        w = wall[s]
+        wall_out[s] = w
+        sel = jnp.where(w >= 0.0, 1.0, 0.0)
+        rank = jnp.where(w >= 0.0, jnp.dot(sel.astype(BF16), before, preferred_element_type=F32), -1.0)
+        rank_ref[s] = rank.astype(jnp.int32)
+        count = jnp.sum(sel, axis=1, keepdims=True).astype(jnp.int32)
+        cnt_ref[s] = jnp.broadcast_to(count, (NE, 128))
+        wide = jnp.broadcast_to(count, (NE, KC))
+        start = jnp.zeros((1, KC), jnp.int32)
+        local_row = []
+        for e in range(NE):
+            n = wide[e:e + 1]
+            at = row - start
+            local_row.append(jnp.where((at >= 0) & (at < n), at, -2).astype(F32))
+            start = start + (n + (G - 1)) // G * G
+        pad = jnp.zeros((128 - NE, SB), F32)
+        cols_buf[0] = jnp.concatenate([rank, pad], axis=0).T
+        cols_buf[1] = jnp.concatenate([w, pad], axis=0).T
+        if s >= 2:
+            puts[s - 2].wait()
+
+        def fill(tb, _, slot=slot, local_row=local_row):
+            toks = pl.ds(pl.multiple_of(tb * 32, 32), 32)
+            rk = cols_buf[0, toks, :]
+            wt = cols_buf[1, toks, :]
+            total = jnp.zeros((32, KC), F32)
+            for e in range(NE):
+                total = jnp.where(rk[:, e:e + 1] == local_row[e], wt[:, e:e + 1], total)
+            hi = total.astype(BF16)
+            rest = total - hi.astype(F32)
+            mid = rest.astype(BF16)
+            ptbuf[slot, 0, toks, :] = hi
+            ptbuf[slot, 1, toks, :] = mid
+            ptbuf[slot, 2, toks, :] = (rest - mid.astype(F32)).astype(BF16)
+            return 0
+
+        lax.fori_loop(0, SB // 32, fill, 0)
+        puts.append(pltpu.make_async_copy(ptbuf.at[slot], pt.at[s], psem.at[slot]))
+        puts[s].start()
     second[0].wait_recv()
     second[1].wait_recv()
     fourth = [relay(12, diag, 0, pn), relay(13, diag, 1, pn)]
@@ -485,9 +571,10 @@
     for c in (*first, *second, *third, *fourth):
         c.wait_send()
     for c in small:
-        c.wait()
-    for c in keep:
-        c.wait()
+        c.wait_send()
+    keep[0].wait()
+    puts[2].wait()
+    puts[3].wait()
 
 
 def gather_call(b, wts, w1, w3, w2):
@@ -495,10 +582,20 @@
     vmem = pl.BlockSpec(memory_space=pltpu.VMEM)
     return pl.pallas_call(
         gather_kernel,
-        out_shape=(jax.ShapeDtypeStruct((8 * T, D), BF16), jax.ShapeDtypeStruct((NSB, NE, SB), F32), jax.ShapeDtypeStruct((T, D), BF16)),
+        out_shape=(
+            jax.ShapeDtypeStruct((8 * T, D), BF16),
+            jax.ShapeDtypeStruct((NSB, NE, SB), F32),
+            jax.ShapeDtypeStruct((NSB, NE, SB), jnp.int32),
+            jax.ShapeDtypeStruct((NSB, NE, 128), jnp.int32),
+            jax.ShapeDtypeStruct((NSB, 3, SB, KC), BF16),
+            jax.ShapeDtypeStruct((T, D), BF16),
+        ),
         in_specs=[any_spec, vmem, vmem, any_spec, any_spec, any_spec],
-        out_specs=(any_spec, any_spec, vmem),
+        out_specs=(any_spec, vmem, vmem, vmem, any_spec, vmem),
         scratch_shapes=[
+            pltpu.VMEM((NSB, NE, SB), F32),
+            pltpu.VMEM((2, 3, SB, KC), BF16),
+            pltpu.VMEM((2, SB, 128), F32),
             pltpu.VMEM((3, 2, D, SF), BF16),
             pltpu.VMEM((3, SF, D), BF16),
             pltpu.VMEM((T, D), F32),
@@ -508,6 +605,7 @@
             pltpu.SemaphoreType.DMA((7,)),
             pltpu.SemaphoreType.DMA((2,)),
             pltpu.SemaphoreType.DMA((3, 3)),
+            pltpu.SemaphoreType.DMA((2,)),
         ],
         compiler_params=pltpu.CompilerParams(collective_id=0, has_side_effects=True, vmem_limit_bytes=VMEM_LIMIT),
         cost_estimate=pl.CostEstimate(flops=12_000_000_000, bytes_accessed=60_000_000, transcendentals=0),
@@ -515,16 +613,20 @@
     )(b, b, wts, w1, w3, w2)
 
 
-def return_kernel(mine, theirs, y_ref, s_ref, out_ref, own, r1, r2x, r2y, r3x, r3y, send, recv, load):
+def return_kernel(table, pt, h, w2, mine, theirs, y_ref, s_ref, out_ref, ptv, hv, wbuf, ebuf, kbuf, own, give, r1, r2x, r2y, r3x, r3y, send, recv, load, wsem, hsem, psem):
     me, pn, xn, yn = neighbours()
     half = T // 2
     top, low = pl.ds(0, half), pl.ds(half, half)
 
     def load_of(j):
-        return pltpu.make_async_copy(mine.at[j], own.at[j], load.at[j])
+        return (pltpu.make_async_copy(theirs.at[j], give.at[lax.rem(j, 3)], load.at[0, j]), pltpu.make_async_copy(mine.at[j], own.at[j], load.at[1, j]))
+
+    def w_of(st):
+        cols = pl.ds(pl.multiple_of((st // NE) * RC, RC), RC)
+        return pltpu.make_async_copy(w2.at[lax.rem(st, NE), :, cols], wbuf.at[lax.rem(st, WS)], wsem.at[lax.rem(st, WS)])
 
     def core_of(j):
-        return remote(theirs.at[j], r1.at[j], send.at[0, j], recv.at[0, j], pn)
+        return remote(give.at[lax.rem(j, 3)], r1.at[j], send.at[0, j], recv.at[0, j], pn)
 
     def x_of(j):
         return remote(own.at[j, pl.ds(1, 2), top, :], r2x.at[j], send.at[1, j], recv.at[1, j], xn)
@@ -545,12 +647,67 @@
 
         lax.fori_loop(0, NC, run, 0)
 
+    over = jnp.full((T, RC), table[NSB * NK], jnp.int32) > 0
+
     def begin(j):
-        load_of(j).start()
+        for c in load_of(j):
+            c.start()
+
+    def add_up(buf, at, first_tok):
+        toks = pl.ds(pl.multiple_of(first_tok, T), T)
+
+        def block(s, _):
+            dx = lax.rem(lax.rem(s, 2) + lax.rem(me // 2, 2), 2)
+            dy = lax.rem(s // 2 + me // 4, 2)
+            place = dx + 3 * dy - 2 * dx * dy
+            ek = kbuf[pl.ds(pl.multiple_of(s * KC, KC), KC), :]
+            total = jnp.dot(ptv[s, 0, toks, :], ek, preferred_element_type=F32)
+            for i in range(1, 3):
+                total = total + jnp.dot(ptv[s, i, toks, :], ek, preferred_element_type=F32)
+            buf[at, place] = jnp.where(over, buf[at, place], total)
+            return 0
+
+        lax.fori_loop(0, NSB, block, 0)
+
+    def make(j):
+        def expert(e, _):
+            st = j * NE + e
+
+            @pl.when(j == 0)
+            def _():
+                h_of(e).wait()
+
+            w_of(st).wait()
+            res = jnp.dot(hv[e], wbuf[lax.rem(st, WS)], preferred_element_type=F32).astype(BF16)
+            ebuf[pl.ds(e * (LM // G), LM // G)] = res.reshape(LM // G, G, RC)
+
+            @pl.when(st + WS < NC * NE)
+            def _():
+                w_of(st + WS).start()
+
+            return 0
+
+        lax.fori_loop(0, NE, expert, 0)
+
+        def move(k, _):
+            for i in range(8):
+                kbuf[pl.ds(pl.multiple_of((k * 8 + i) * G, G), G), :] = ebuf[table[k * 8 + i]]
+            return 0
+
+        lax.fori_loop(0, NSB * NK // 8, move, 0)
+
+        @pl.when(j == 0)
+        def _():
+            for c in pt_copies:
+                c.wait()
+
+        for c in load_of(j):
+            c.wait()
+        add_up(give, lax.rem(j, 3), T - lax.rem(me, 2) * T)
         core_of(j).start()
+        add_up(own, j, lax.rem(me, 2) * T)
 
     def pair(j):
-        load_of(j).wait()
         core_of(j).wait_recv()
         own[j, 1:] = own[j, 1:] + r1[j, 1:]
         x_of(j).start()
@@ -574,28 +731,71 @@
         out_ref[half:, cols] = (base[half:] + (own[j, 0, half:] + r2y[j, 1] + r3x[j])).astype(BF16)
 
     def drain(j):
-        for c in (core_of(j), x_of(j), y_of(j), y_last(j), x_last(j)):
+        for c in (x_of(j), y_of(j), y_last(j), x_last(j)):
             c.wait_send()
 
+    def h_of(e):
+        return pltpu.make_async_copy(h.at[e, pl.ds(0, LM), :], hv.at[e], hsem.at[e])
+
+    pt_copies = [pltpu.make_async_copy(pt.at[s], ptv.at[s], psem.at[s]) for s in range(NSB)]
+    for e in range(NE):
+        h_of(e).start()
+        if e < WS:
+            w_of(e).start()
+    begin(0)
+    begin(1)
+    for c in pt_copies:
+        c.start()
+    ebuf[NOROW] = jnp.zeros((G, RC), BF16)
     enter([pn, xn, yn])
-    each(begin)
-    each(pair)
-    each(onward)
+
+    def steady(j, _):
+        @pl.when(j >= 2)
+        def _():
+            core_of(j - 2).wait_send()
+
+        @pl.when((j >= 1) & (j + 1 < NC))
+        def _():
+            begin(j + 1)
+
+        make(j)
+        pair(j)
+
+        @pl.when(j >= LAG)
+        def _():
+            onward(j - LAG)
+
+        return 0
+
+    lax.fori_loop(0, NC, steady, 0)
+
+    def last(j, _):
+        core_of(j).wait_send()
+        onward(j)
+        return 0
+
+    lax.fori_loop(NC - LAG, NC, last, 0)
     each(finish)
     each(drain)
 
 
-def return_call(mine, theirs, hidden, shared_out):
+def return_call(table, pt, h, w2, mine, theirs, hidden, shared_out):
     any_spec = pl.BlockSpec(memory_space=pl.ANY)
     vmem = pl.BlockSpec(memory_space=pltpu.VMEM)
     half = T // 2
     return pl.pallas_call(
         return_kernel,
         out_shape=jax.ShapeDtypeStruct((T, D), BF16),
-        in_specs=[any_spec, any_spec, vmem, vmem],
+        in_specs=[pl.BlockSpec(memory_space=pltpu.SMEM), any_spec, any_spec, any_spec, any_spec, any_spec, vmem, vmem],
         out_specs=vmem,
         scratch_shapes=[
+            pltpu.VMEM((NSB, 3, SB, KC), BF16),
+            pltpu.VMEM((NE, LM, FF), BF16),
+            pltpu.VMEM((WS, FF, RC), BF16),
+            pltpu.VMEM((NOROW + 1, G, RC), BF16),
+            pltpu.VMEM((NSB * KC, RC), BF16),
             pltpu.VMEM((NC, NSB, T, RC), F32),
+            pltpu.VMEM((3, NSB, T, RC), F32),
             pltpu.VMEM((NC, NSB, T, RC), F32),
             pltpu.VMEM((NC, 2, half, RC), F32),
             pltpu.VMEM((NC, 2, half, RC), F32),
@@ -603,11 +803,14 @@
             pltpu.VMEM((NC, half, RC), F32),
             pltpu.SemaphoreType.DMA((5, NC)),
             pltpu.SemaphoreType.DMA((5, NC)),
-            pltpu.SemaphoreType.DMA((NC,)),
+            pltpu.SemaphoreType.DMA((2, NC)),
+            pltpu.SemaphoreType.DMA((WS,)),
+            pltpu.SemaphoreType.DMA((NE,)),
+            pltpu.SemaphoreType.DMA((NSB,)),
         ],
         compiler_params=pltpu.CompilerParams(collective_id=1, has_side_effects=True, vmem_limit_bytes=VMEM_LIMIT),
         name="return_sum",
-    )(mine, theirs, hidden, shared_out)
+    )(table, pt, h, w2, mine, theirs, hidden, shared_out)
 
 
 def solution(mesh):
@@ -619,19 +822,15 @@
         probs = jax.nn.softmax(jnp.dot(normed, w_gate, preferred_element_type=F32), axis=-1)
         chosen = jnp.any(topk_ids[:, :, None] == jnp.arange(EXPERTS), axis=1)
         gate_wts = jnp.where(chosen, ROUTE_SCALE * probs, -1.0).T
-        ball, wsb, shared_out = gather_call(normed, gate_wts, w1_shared, w3_shared, w2_shared)
+        ball, wsb, rank, counts, pt, shared_out = gather_call(normed, gate_wts, w1_shared, w3_shared, w2_shared)
+        cnt = counts[:, :, 0]
         me = lax.axis_index('ep')
-        sel = wsb >= 0.0
-        cnt = jnp.sum(sel, axis=2, dtype=jnp.int32)
-        before = jnp.arange(SB)[:, None] < jnp.arange(SB)[None, :]
-        rank = jnp.einsum('set,tu->seu', sel.astype(BF16), before.astype(BF16), preferred_element_type=F32)
-        rank = jnp.where(sel, rank.astype(jnp.int32), -1)
         chip, at = me // 2, jnp.arange(NSB)
         other_x, other_y = at % 2 != chip % 2, at // 2 != chip // 2
         place = jnp.where(other_x, jnp.where(other_y, 2, 1), jnp.where(other_y, 3, 0))
         core = jnp.concatenate([(me % 2)[None], place]).astype(jnp.int32)
-        h = up_call(cnt, rank, ball, w1_experts, w3_experts)
-        mine, theirs = down_call(cnt, core, rank, wsb, h, w2_experts)
-        return return_call(mine, theirs, hidden, shared_out)
+        h, table = up_call(cnt, rank, ball, w1_experts, w3_experts)
+        mine, theirs = down_call(table, cnt, core, rank, wsb, h, w2_experts)
+        return return_call(table, pt, h, w2_experts, mine, theirs, hidden, shared_out)
 
     return jax.shard_map(local_fn, mesh=mesh, in_specs=(tok_spec, P(), P(), P(), P(), P(), expert_spec, expert_spec, expert_spec, tok_spec), out_specs=tok_spec, check_vma=False)

time: 297 us -> 243 us (0.82)
  Pallas kernels: 284 us -> 232 us
    pallas_call x2, Pallas kernels: 131 us -> 59 us  [the longest x1 58 us: up_call(): pl.pallas_call(up_kernel, out_shape=(jax.ShapeDtypeStruct((NE, HR, FF), B...]
    pallas_call x1, Pallas kernels: 98.5 us -> 118 us  [return_call(): pl.pallas_call(return_kernel, out_shape=jax.ShapeDtypeStruct((T, D), BF16...]
where the time goes in v4:
time: 243 us
  Pallas kernels  232 us (95%)
  other arithmetic  6.08 us (3%)
  local copies, waits for them, and re-layouts  4.96 us (2%)
    pallas_call x1, Pallas kernels, return_call(): pl.pallas_call(return_kernel, out_shape=jax.ShapeDtypeStruct((T, D), BF16...  118 us
    pallas_call x1, Pallas kernels, up_call(): pl.pallas_call(up_kernel, out_shape=(jax.ShapeDtypeStruct((NE, HR, FF), B...  58 us
    pallas_call x1, Pallas kernels, gather_call(): pl.pallas_call(gather_kernel, out_shape=(jax.ShapeDtypeStruct((8 * T, D),...  54.2 us

profile of v4, /device:TPU:0, one launch (start us, length us, event | category | flops | bytes accessed | tf_op | source)
XLA Modules:
  0.0 243.2 jit_solution(12673270188986260923)
XLA Ops:
  0.0 0.0 copy-start
  0.0 0.6 pad_add_fusion.core_ref
  0.6 1.7 fusion
  2.3 0.7 convert_element_type.10
  3.0 0.7 fusion.3
  3.7 1.7 fusion.2.b_any.b_ref
  5.4 0.0 copy-start.2
  5.4 1.0 copy-done.2
  6.5 0.0 copy-done
  6.5 0.5 fusion.5
  7.0 0.6 select_bitcast_fusion.wts_ref
  7.7 54.2 %gather.1 = (bf16[2048,2560]{1,0:T(8,128)(2,1)}, f32[4,8,512]{2,1,0:T(8,128)}, s32[4,8,512]{2,1,0:T(8,128)}, s32[4,8,128]{2,1,0:T(8,128)}, bf16[4,3,512,768]{3,2,1,0:T(8,128)(2,1)}, /*index=5*/bf16[256,2560]{1,0:T(8,128)(2,1)}) custom-call(bf16[256,2560]{1,0:T(8,128)(2,1)} %copy-done.2, bf16[256,2560]{1,0:T(8,128)(2,1)} %copy-done.2, ...), custom_call_target="tpu_custom_call" | custom-call | flops 12000000000 | bytes 60000000 | tf_op jit(solution)/shard_map/gather/pallas_call | solution.py:583
  61.9 1.4 slice_reduce_fusion.cnt_ref
  63.4 58.0 %up.1 = (bf16[8,1280,1536]{2,1,0:T(8,128)(2,1)}, s32[256]{0:T(256)}) custom-call(s32[4,8]{1,0:T(4,128)} %slice_reduce_fusion.cnt_ref, s32[4,8,512]{2,1,0:T(8,128)} %get-tuple-element.16.rank_ref, bf16[2048,2560]{1,0:T(8,128)(2,1)} %get-tuple-element.17.ball, bf16[8,2560,1536]{2,1,0:T(8,128)(2,1)} %w1.3, bf16[8,2560,1536]{2,1,0:T(8,128)(2,1)} %w3.3), custom_call_target="tpu_custom_call" | custom-call | flops 48000000000 | bytes 140000000 | tf_op jit(solution)/shard_map/up/pallas_call | solution.py:213
  121.3 1.0 down.1
  122.4 0.0 copy-start.1
  122.4 118.4 %return_sum.1 = bf16[256,2560]{1,0:T(8,128)(2,1)} custom-call(s32[256]{0:T(256)} %get-tuple-element.18.table, bf16[4,3,512,768]{3,2,1,0:T(8,128)(2,1)} %get-tuple-element.19.pt, bf16[8,1280,1536]{2,1,0:T(8,128)(2,1)} %get-tuple-element.20.h, bf16[8,1536,2560]{2,1,0:T(8,128)(2,1)} %w2.5, f32[10,4,256,256]{3,2,1,0:T(8,128)} %get-tuple-element.22.mine, ...), custom_call_target="tpu_custom_call" | custom-call | tf_op jit(solution)/shard_map/return_sum/pallas_call | solution.py:786
  240.8 2.5 %copy.14 = bf16[256,2560]{1,0:T(8,128)(2,1)} copy(bf16[256,2560]{1,0:T(8,128)(2,1)} %return_sum.1) | data formatting | bytes 2621440
  243.2 0.0 copy-done.1
  (3 shorter events, 0.1 us)
Async XLA Ops:
  0.0 6.5 %copy-start = (bf16[2560,64]{0,1:T(8,128)(2,1)S(1)}, bf16[2560,64]{0,1:T(8,128)(2,1)}, u32[]{:S(2)}) copy-start(bf16[2560,64]{0,1:T(8,128)(2,1)} %param.12) | copy-start | bytes 983044
  5.4 1.1 copy-start.2
  122.4 120.9 %copy-start.1 = (bf16[2560,64]{0,1:T(8,128)(2,1)S(1)}, bf16[2560,64]{0,1:T(8,128)(2,1)}, u32[]{:S(2)}) copy-start(bf16[2560,64]{0,1:T(8,128)(2,1)} %param.12) | copy-start | bytes 983044

commit v5 on v4

--- a/solution.py
+++ b/solution.py
@@ -42,12 +42,6 @@
 F32 = jnp.float32
 
 
-def rms_norm(hidden, norm_gain):
-    rows_f = hidden.astype(F32)
-    inv_rms = lax.rsqrt(jnp.mean(rows_f * rows_f, axis=-1, keepdims=True) + NORM_EPS)
-    return (rows_f * inv_rms * norm_gain.astype(F32)).astype(BF16)
-
-
 def offsets(cnt_ref, ng, eoff, est, boff, nsb_g):
     run = jnp.int32(0)
     for e in range(NE):
@@ -441,7 +435,7 @@
     pl.semaphore_wait(barrier, len(others))
 
 
-def gather_kernel(b_any, b_ref, wts_ref, w1, w3, w2, ball, wall_out, rank_ref, cnt_ref, pt, s_ref, wall, ptbuf, cols_buf, w13buf, w2buf, acc, send, recv, wsend, wrecv, local, wsem, psem):
+def gather_kernel(y_ref, gain_ref, wg_ref, ids_ref, w1, w3, w2, ball, wall_out, rank_ref, cnt_ref, pt, s_ref, b_ref, wts_ref, wall, ptbuf, cols_buf, w13buf, w2buf, acc, send, recv, wsend, wrecv, local, wsem, psem):
     me, pn, xn, yn = neighbours()
     diag = xn + yn - me
     half = T // 2
@@ -450,7 +444,7 @@
         return pl.ds(pl.multiple_of(dev * T + h * half, half), half)
 
     def own(k, h, dev):
-        return remote(b_any.at[pl.ds(h * half, half), :], ball.at[rows(me, h), :], send.at[k], recv.at[k], dev)
+        return remote(b_ref.at[pl.ds(h * half, half), :], ball.at[rows(me, h), :], send.at[k], recv.at[k], dev)
 
     def relay(k, owner, h, dev):
         return remote(ball.at[rows(owner, h), :], ball.at[rows(owner, h), :], send.at[k], recv.at[k], dev)
@@ -464,6 +458,24 @@
     for st in range(3):
         for c in w_copies(st, st):
             c.start()
+    def norm(i, _):
+        block = pl.ds(pl.multiple_of(i * 16, 16), 16)
+        rows_f = y_ref[block, :].astype(F32)
+        inv_rms = lax.rsqrt(jnp.mean(rows_f * rows_f, axis=-1, keepdims=True) + NORM_EPS)
+        b_ref[block, :] = (rows_f * inv_rms * gain_ref[...].astype(F32)).astype(BF16)
+        return 0
+
+    lax.fori_loop(0, T // 16, norm, 0)
+    logits = jnp.dot(b_ref[...], wg_ref[...], preferred_element_type=F32)
+    raised = jnp.exp(logits - jnp.max(logits, axis=-1, keepdims=True))
+    probs = raised / jnp.sum(raised, axis=-1, keepdims=True)
+    ids = ids_ref[...]
+    expert_id = lax.broadcasted_iota(jnp.int32, (T, EXPERTS), 1)
+    chosen = ids[:, 0:1] == expert_id
+    for k in range(1, ids.shape[1]):
+        chosen = chosen | (ids[:, k:k + 1] == expert_id)
+    gate_wts = jnp.where(chosen, ROUTE_SCALE * probs, -1.0)
+    wts_ref[...] = jnp.concatenate([gate_wts, gate_wts], axis=1).T[:EXPERTS]
     others = [lax.rem(me + k, 8) for k in range(1, 8)]
     enter(others)
     first = [own(0, 0, xn), own(2, 1, yn), own(1, 1, xn), own(3, 0, yn), own(4, 0, pn), own(5, 1, pn)]
@@ -577,7 +589,7 @@
     puts[3].wait()
 
 
-def gather_call(b, wts, w1, w3, w2):
+def gather_call(y, gain, wg, ids, w1, w3, w2):
     any_spec = pl.BlockSpec(memory_space=pl.ANY)
     vmem = pl.BlockSpec(memory_space=pltpu.VMEM)
     return pl.pallas_call(
@@ -590,9 +602,11 @@
             jax.ShapeDtypeStruct((NSB, 3, SB, KC), BF16),
             jax.ShapeDtypeStruct((T, D), BF16),
         ),
-        in_specs=[any_spec, vmem, vmem, any_spec, any_spec, any_spec],
+        in_specs=[vmem, vmem, vmem, vmem, any_spec, any_spec, any_spec],
         out_specs=(any_spec, vmem, vmem, vmem, any_spec, vmem),
         scratch_shapes=[
+            pltpu.VMEM((T, D), BF16),
+            pltpu.VMEM((EXPERTS, T), F32),
             pltpu.VMEM((NSB, NE, SB), F32),
             pltpu.VMEM((2, 3, SB, KC), BF16),
             pltpu.VMEM((2, SB, 128), F32),
@@ -610,7 +624,7 @@
         compiler_params=pltpu.CompilerParams(collective_id=0, has_side_effects=True, vmem_limit_bytes=VMEM_LIMIT),
         cost_estimate=pl.CostEstimate(flops=12_000_000_000, bytes_accessed=60_000_000, transcendentals=0),
         name="gather",
-    )(b, b, wts, w1, w3, w2)
+    )(y, gain, wg, ids, w1, w3, w2)
 
 
 def return_kernel(table, pt, h, w2, mine, theirs, y_ref, s_ref, out_ref, ptv, hv, wbuf, ebuf, kbuf, own, give, r1, r2x, r2y, r3x, r3y, send, recv, load, wsem, hsem, psem):
@@ -818,11 +832,7 @@
     expert_spec = P('ep', None, None)
 
     def local_fn(hidden, norm_gain, w_gate, w1_shared, w3_shared, w2_shared, w1_experts, w3_experts, w2_experts, topk_ids):
-        normed = rms_norm(hidden, norm_gain)
-        probs = jax.nn.softmax(jnp.dot(normed, w_gate, preferred_element_type=F32), axis=-1)
-        chosen = jnp.any(topk_ids[:, :, None] == jnp.arange(EXPERTS), axis=1)
-        gate_wts = jnp.where(chosen, ROUTE_SCALE * probs, -1.0).T
-        ball, wsb, rank, counts, pt, shared_out = gather_call(normed, gate_wts, w1_shared, w3_shared, w2_shared)
+        ball, wsb, rank, counts, pt, shared_out = gather_call(hidden, norm_gain.reshape(1, D), w_gate, topk_ids, w1_shared, w3_shared, w2_shared)
         cnt = counts[:, :, 0]
         me = lax.axis_index('ep')
         chip, at = me // 2, jnp.arange(NSB)

time: 243 us -> 245 us (level)
  other arithmetic: 6.08 us -> 0.66 us
  local copies, waits for them, and re-layouts: 4.96 us -> 8.73 us
    pallas_call x1, Pallas kernels: 54.2 us -> 57.2 us  [gather_call(): pl.pallas_call(gather_kernel, out_shape=(jax.ShapeDtypeStruct((8 * T, D),...]
    unnamed x7 -> x3, local copies, waits for them, and re-layouts: 3.52 us -> 6 us
where the time goes in v5:
time: 245 us; the launch traced here: 243 us
  Pallas kernels  234 us (96%)
  local copies, waits for them, and re-layouts  8.73 us (4%)
    pallas_call x1, Pallas kernels, return_call(): pl.pallas_call(return_kernel, out_shape=jax.ShapeDtypeStruct((T, D), BF16...  117 us
    pallas_call x1, Pallas kernels, up_call(): pl.pallas_call(up_kernel, out_shape=(jax.ShapeDtypeStruct((NE, HR, FF), B...  59.1 us
    pallas_call x1, Pallas kernels, gather_call(): pl.pallas_call(gather_kernel, out_shape=(jax.ShapeDtypeStruct((8 * T, D),...  57.2 us
    unnamed x3, local copies, waits for them, and re-layouts  6 us

profile of v5, /device:TPU:0, one launch (start us, length us, event | category | flops | bytes accessed | tf_op | source)
XLA Modules:
  0.0 243.4 jit_solution(8522480130092413050)
XLA Ops:
  0.0 0.7 pad_add_fusion.core_ref
  0.7 1.3 reshape.3.gain_ref
  2.0 1.5 copy.14.ids_ref
  3.4 2.1 copy.13.wg_ref
  5.5 57.2 %gather.1 = (bf16[2048,2560]{1,0:T(8,128)(2,1)}, f32[4,8,512]{2,1,0:T(8,128)}, s32[4,8,512]{2,1,0:T(8,128)}, s32[4,8,128]{2,1,0:T(8,128)}, bf16[4,3,512,768]{3,2,1,0:T(8,128)(2,1)}, /*index=5*/bf16[256,2560]{1,0:T(8,128)(2,1)}) custom-call(bf16[256,2560]{1,0:T(8,128)(2,1)} %y_ref.3, bf16[1,2560]{1,0:T(2,128)(2,1)} %reshape.3.gain_ref, ...), custom_call_target="tpu_custom_call" | custom-call | flops 12000000000 | bytes 60000000 | tf_op jit(solution)/shard_map/gather/pallas_call | solution.py:595
  62.7 1.4 slice_reduce_fusion.cnt_ref
  64.2 59.1 %up.1 = (bf16[8,1280,1536]{2,1,0:T(8,128)(2,1)}, s32[256]{0:T(256)}) custom-call(s32[4,8]{1,0:T(4,128)} %slice_reduce_fusion.cnt_ref, s32[4,8,512]{2,1,0:T(8,128)} %get-tuple-element.16.rank_ref, bf16[2048,2560]{1,0:T(8,128)(2,1)} %get-tuple-element.17.ball, bf16[8,2560,1536]{2,1,0:T(8,128)(2,1)} %w1.3, bf16[8,2560,1536]{2,1,0:T(8,128)(2,1)} %w3.3), custom_call_target="tpu_custom_call" | custom-call | flops 48000000000 | bytes 140000000 | tf_op jit(solution)/shard_map/up/pallas_call | solution.py:207
  123.2 1.0 down.1
  124.2 116.7 %return_sum.1 = bf16[256,2560]{1,0:T(8,128)(2,1)} custom-call(s32[256]{0:T(256)} %get-tuple-element.18.table, bf16[4,3,512,768]{3,2,1,0:T(8,128)(2,1)} %get-tuple-element.19.pt, bf16[8,1280,1536]{2,1,0:T(8,128)(2,1)} %get-tuple-element.20.h, bf16[8,1536,2560]{2,1,0:T(8,128)(2,1)} %w2.5, f32[10,4,256,256]{3,2,1,0:T(8,128)} %get-tuple-element.22.mine, ...), custom_call_target="tpu_custom_call" | custom-call | tf_op jit(solution)/shard_map/return_sum/pallas_call | solution.py:800
  240.9 2.5 %copy.16 = bf16[256,2560]{1,0:T(8,128)(2,1)} copy(bf16[256,2560]{1,0:T(8,128)(2,1)} %return_sum.1) | data formatting | bytes 2621440
  (1 shorter events, 0.0 us)
